TPU v7x, 16 devices: a whole 2x2x2 slice. The times are simulated.
16 devices in a mesh: right: 4 (over z, y), left: 4 (over x, core).
Axes of the slice: x: 2, y: 2, z: 2, core: 2. Of those that a mesh axis runs over, the one named last changes fastest.
Arguments:
- psi_init: float32 [2048, 2, 2, 512], P('left', None, None, 'right')
- left_env: float32 [2048, 20, 2048], P('left')
- right_env: float32 [512, 20, 512], P('right')
- mpo_two: float32 [20, 20, 2, 2, 2, 2], replicated
Outputs:
- output 1: float32 [4], replicated
- output 2: float32 [4], replicated
- output 3: float32 [2048, 2, 2, 512], P('left', None, None, 'right')
All inputs are finite; a program needn't handle non-finite values.
Results may differ from a plain program's by a relative error of at most 0.001.
Values sent between devices are 32-bit elements.
A program may use at most 1 GiB of HBM per device.

v0:
```python
import jax
import jax.numpy as jnp
from jax import lax
from jax.sharding import PartitionSpec as P

LANCZOS_STEPS = 4
PREC_HIGH = lax.Precision.HIGHEST


def solution(mesh):
    device_count = mesh.shape['left'] * mesh.shape['right']

    def global_dot(vec_one, vec_two):
        return lax.psum(jnp.sum(vec_one * vec_two), ('left', 'right'))

    def apply_ham(vec_block, env_cols, env_right, mpo_two):
        gathered = lax.all_gather(vec_block, 'left', axis=0, tiled=True)
        t_one = jnp.einsum('alc,astb->lcstb', env_cols, gathered, precision=PREC_HIGH, preferred_element_type=jnp.float32)
        t_two = jnp.einsum('lcstb,lrstuv->cbruv', t_one, mpo_two, precision=PREC_HIGH, preferred_element_type=jnp.float32)
        partial_out = jnp.einsum('cbruv,brd->cuvd', t_two, env_right, precision=PREC_HIGH, preferred_element_type=jnp.float32)
        return lax.psum_scatter(partial_out, 'right', scatter_dimension=3, tiled=True)

    def lanczos(psi_block, left_env, right_env, mpo_two):
        env_cols = lax.all_to_all(left_env, 'left', split_axis=2, concat_axis=0, tiled=True)
        elem_count = psi_block.size * device_count
        vec_cur = psi_block * jnp.sqrt(elem_count / global_dot(psi_block, psi_block))
        vec_prev = vec_cur
        beta_prev = jnp.float32(0.0)
        alpha_list = []
        beta_list = []
        for step_idx in range(LANCZOS_STEPS):
            next_vec = apply_ham(vec_cur, env_cols, right_env, mpo_two)
            alpha_val = global_dot(vec_cur, next_vec) / elem_count
            next_vec = next_vec - alpha_val * vec_cur
            if step_idx > 0:
                next_vec = next_vec - beta_prev * vec_prev
            beta_val = jnp.sqrt(global_dot(next_vec, next_vec) / elem_count)
            vec_prev = vec_cur
            vec_cur = next_vec / beta_val
            beta_prev = beta_val
            alpha_list.append(alpha_val)
            beta_list.append(beta_val)
        return jnp.stack(alpha_list), jnp.stack(beta_list), vec_cur

    return jax.shard_map(
        lanczos,
        mesh=mesh,
        in_specs=(P('left', None, None, 'right'), P('left', None, None), P('right', None, None), P()),
        out_specs=(P(), P(), P('left', None, None, 'right')),
        check_vma=False,
    )
```

profile of v0, /device:TPU:0, one launch (start us, length us, event | category | flops | bytes accessed | tf_op | source)
XLA Modules:
  0.0 2894.0 jit_solution(10224890509204309612)
XLA Ops:
  7.2 92.5 %copy.32 = f32[512,20,2048]{0,1,2:T(8,128)} copy(f32[512,20,2048]{2,0,1:T(8,128)} %param.5) | data formatting | bytes 167772160 | tf_op args[1]
  99.6 18.8 all-to-all-start
  118.4 0.0 all-gather.5.cloned.1.call-start
  118.5 1.7 multiply_reduce_fusion.8
  120.2 1107.3 %psum.63 = f32[]{:T(128)} all-reduce(f32[]{:T(128)} %multiply_reduce_fusion.8), channel_id=1, replica_groups=mesh['right'=4,'left'=4] {'left','right'}, use_global_device_ids=true, to_apply=%region_1.0 | all-reduce | flops 1 | bytes 8 | tf_op jit(solution)/shard_map/psum | solution.py:14
  1227.5 0.8 copy.31
  1229.0 1.1 broadcast_multiply_fusion
  1230.1 0.0 all-gather.5.cloned.1.call-update
  1230.2 0.0 reduce-scatter.5.cloned.1.call-start
  1230.2 0.2 copy.36
  1230.5 90.0 %copy.34 = f32[4,512,20,512]{3,1,0,2:T(8,128)} copy(f32[4,512,20,512]{1,2,3,0:T(8,128)} %bitcast.4) | data formatting | bytes 167772160 | tf_op jit(solution)/shard_map/all_to_all | solution.py:24
  1320.4 146.7 %convolution_bitcast_fusion.7 = f32[20,512,2,2,128,1,1]{1,4,0,3,2,6,5:T(8,128)} fusion(f32[2048,20,512,1,1]{2,0,1,4,3:T(8,128)} %bitcast.7, f32[2048,2,2,128]{0,3,2,1:T(8,128)} %all-gather.5.cloned.1.call-done), kind=kOutput, calls=%fused_computation.15 | convolution fusion | flops 128849018880 | bytes 109051904 | tf_op jit(solution)/shard_map/alc,astb->lcstb/dot_general | solution.py:18
  1467.2 23.7 copy.54
  1490.9 28.9 convolution_bitcast_fusion.3
  1519.8 46.5 %fusion.16 = f32[512,2,2,512]{0,3,2,1:T(8,128)} fusion(f32[128,20,512]{2,0,1:T(8,128)} %param.6, f32[512,128,20,2,2]{1,2,4,3,0:T(8,128)} %convolution_bitcast_fusion.3), kind=kOutput, calls=%fused_computation.24 | convolution fusion | flops 32212254720 | bytes 30408704 | tf_op jit(solution)/shard_map/cbruv,brd->cuvd/dot_general | solution.py:20
  1566.3 0.0 all-gather.7.cloned.1.call-start
  1566.4 49.6 %reduce-scatter.5.cloned.1.call-done = f32[512,2,2,128]{0,3,2,1:T(8,128)} async-done(((f32[512,2,2,512]{0,3,2,1:T(8,128)}), f32[512,2,2,128]{0,3,2,1:T(8,128)}) %reduce-scatter.5.cloned.1.call-update) | async-done | bytes 1048592 | tf_op jit(solution)/shard_map/reduce_scatter | solution.py:21
  1616.0 2.1 multiply_reduce_fusion.7
  1618.1 31.9 %psum.64 = f32[]{:T(128)} all-reduce(f32[]{:T(128)} %multiply_reduce_fusion.7), channel_id=1, replica_groups=mesh['right'=4,'left'=4] {'left','right'}, use_global_device_ids=true, to_apply=%region_4.0 | all-reduce | flops 1 | bytes 8 | tf_op jit(solution)/shard_map/psum | solution.py:14
  1650.6 2.1 multiply_reduce_fusion.6
  1652.7 32.7 %psum.65 = f32[]{:T(128)} all-reduce(f32[]{:T(128)} %multiply_reduce_fusion.6), channel_id=1, replica_groups=mesh['right'=4,'left'=4] {'left','right'}, use_global_device_ids=true, to_apply=%region_6.0 | all-reduce | flops 1 | bytes 8 | tf_op jit(solution)/shard_map/psum | solution.py:14
  1686.1 2.4 broadcast_divide_fusion.3
  1688.6 0.0 all-gather.7.cloned.1.call-update
  1688.6 0.0 reduce-scatter.7.cloned.1.call-start
  1688.7 33.3 %all-gather.7.cloned.1.call-done = f32[2048,2,2,128]{0,3,2,1:T(8,128)} async-done(((f32[512,2,2,128]{0,3,2,1:T(8,128)}), f32[2048,2,2,128]{0,3,2,1:T(8,128)}) %all-gather.7.cloned.1.call-update) | async-done | bytes 4194320 | tf_op jit(solution)/shard_map/all_gather | solution.py:17
  1722.0 146.7 %convolution_bitcast_fusion.6 = f32[20,512,2,2,128,1,1]{1,4,0,3,2,6,5:T(8,128)} fusion(f32[2048,20,512,1,1]{2,0,1,4,3:T(8,128)} %bitcast.7, f32[2048,2,2,128]{0,3,2,1:T(8,128)} %all-gather.7.cloned.1.call-done), kind=kOutput, calls=%fused_computation.14 | convolution fusion | flops 128849018880 | bytes 109051904 | tf_op jit(solution)/shard_map/alc,astb->lcstb/dot_general | solution.py:18
  1868.7 23.7 copy.59
  1892.5 28.9 convolution_bitcast_fusion.2
  1921.4 46.6 %fusion.21 = f32[512,2,2,512]{0,3,2,1:T(8,128)} fusion(f32[128,20,512]{2,0,1:T(8,128)} %param.6, f32[512,128,20,2,2]{1,2,4,3,0:T(8,128)} %convolution_bitcast_fusion.2), kind=kOutput, calls=%fused_computation.25 | convolution fusion | flops 32212254720 | bytes 30408704 | tf_op jit(solution)/shard_map/cbruv,brd->cuvd/dot_general | solution.py:20
  1968.0 0.0 all-gather.9.cloned.1.call-start
  1968.0 48.8 %reduce-scatter.7.cloned.1.call-done = f32[512,2,2,128]{0,3,2,1:T(8,128)} async-done(((f32[512,2,2,512]{0,3,2,1:T(8,128)}), f32[512,2,2,128]{0,3,2,1:T(8,128)}) %reduce-scatter.7.cloned.1.call-update) | async-done | bytes 1048592 | tf_op jit(solution)/shard_map/reduce_scatter | solution.py:21
  2016.8 2.1 multiply_reduce_fusion.5
  2018.9 31.9 %psum.66 = f32[]{:T(128)} all-reduce(f32[]{:T(128)} %multiply_reduce_fusion.5), channel_id=1, replica_groups=mesh['right'=4,'left'=4] {'left','right'}, use_global_device_ids=true, to_apply=%region_9.0 | all-reduce | flops 1 | bytes 8 | tf_op jit(solution)/shard_map/psum | solution.py:14
  2051.4 2.1 multiply_reduce_fusion.4
  2053.6 32.7 %psum.67 = f32[]{:T(128)} all-reduce(f32[]{:T(128)} %get-tuple-element.19), channel_id=1, replica_groups=mesh['right'=4,'left'=4] {'left','right'}, use_global_device_ids=true, to_apply=%region_11.0 | all-reduce | flops 1 | bytes 8 | tf_op jit(solution)/shard_map/psum | solution.py:14
  2087.0 1.1 broadcast_divide_fusion.2
  2088.1 0.0 reduce-scatter.9.cloned.1.call-start
  2088.2 33.4 %all-gather.9.cloned.1.call-done = f32[2048,2,2,128]{0,3,2,1:T(8,128)} async-done(((f32[512,2,2,128]{0,3,2,1:T(8,128)}), f32[2048,2,2,128]{0,3,2,1:T(8,128)}) %all-gather.9.cloned.1.call-update) | async-done | bytes 4194320 | tf_op jit(solution)/shard_map/all_gather | solution.py:17
  2121.5 146.7 %convolution_bitcast_fusion.5 = f32[20,512,2,2,128,1,1]{1,4,0,3,2,6,5:T(8,128)} fusion(f32[2048,20,512,1,1]{2,0,1,4,3:T(8,128)} %bitcast.7, f32[2048,2,2,128]{0,3,2,1:T(8,128)} %all-gather.9.cloned.1.call-done), kind=kOutput, calls=%fused_computation.13 | convolution fusion | flops 128849018880 | bytes 109051904 | tf_op jit(solution)/shard_map/alc,astb->lcstb/dot_general | solution.py:18
  2268.3 23.7 copy.63
  2292.0 29.1 %convolution_bitcast_fusion.1 = f32[512,128,20,2,2]{1,2,4,3,0:T(8,128)} fusion(f32[20,512,2,2,128,1,1]{4,0,3,2,6,5,1:T(8,128)} %copy.63, f32[20,20,2,2,2,2]{0,1,3,2,5,4:T(8,128)S(1)} %copy.36), kind=kOutput, calls=%fused_computation.9 | convolution fusion | flops 5033164800 | bytes 41968640 | tf_op jit(solution)/shard_map/lcstb,lrstuv->cbruv/dot_general | solution.py:19
  2321.1 45.0 %fusion.26 = f32[512,2,2,512]{0,3,2,1:T(8,128)} fusion(f32[128,20,512]{2,0,1:T(8,128)S(1)} %bitcast.108, f32[512,128,20,2,2]{1,2,4,3,0:T(8,128)} %convolution_bitcast_fusion.1), kind=kOutput, calls=%fused_computation.26 | convolution fusion | flops 32212254720 | bytes 30408704 | tf_op jit(solution)/shard_map/cbruv,brd->cuvd/dot_general | solution.py:20
  2366.1 0.0 all-gather.11.cloned.1.call-start
  2366.2 48.8 %reduce-scatter.9.cloned.1.call-done = f32[512,2,2,128]{0,3,2,1:T(8,128)} async-done(((f32[512,2,2,512]{0,3,2,1:T(8,128)}), f32[512,2,2,128]{0,3,2,1:T(8,128)}) %reduce-scatter.9.cloned.1.call-update) | async-done | bytes 1048592 | tf_op jit(solution)/shard_map/reduce_scatter | solution.py:21
  2414.9 2.1 multiply_reduce_fusion.3
  2417.0 31.9 %psum.68 = f32[]{:T(128)} all-reduce(f32[]{:T(128)} %multiply_reduce_fusion.3), channel_id=1, replica_groups=mesh['right'=4,'left'=4] {'left','right'}, use_global_device_ids=true, to_apply=%region_14.0 | all-reduce | flops 1 | bytes 8 | tf_op jit(solution)/shard_map/psum | solution.py:14
  2449.6 2.1 multiply_reduce_fusion.2
  2451.7 32.7 %psum.69 = f32[]{:T(128)} all-reduce(f32[]{:T(128)} %get-tuple-element.17), channel_id=1, replica_groups=mesh['right'=4,'left'=4] {'left','right'}, use_global_device_ids=true, to_apply=%region_16.0 | all-reduce | flops 1 | bytes 8 | tf_op jit(solution)/shard_map/psum | solution.py:14
  2485.1 1.1 broadcast_divide_fusion.1
  2486.2 0.0 reduce-scatter.11.cloned.1.call-start
  2486.3 33.4 %all-gather.11.cloned.1.call-done = f32[2048,2,2,128]{0,3,2,1:T(8,128)} async-done(((f32[512,2,2,128]{0,3,2,1:T(8,128)}), f32[2048,2,2,128]{0,3,2,1:T(8,128)}) %all-gather.11.cloned.1.call-update) | async-done | bytes 4194320 | tf_op jit(solution)/shard_map/all_gather | solution.py:17
  2519.6 146.7 %convolution_bitcast_fusion.4 = f32[20,512,2,2,128,1,1]{1,4,0,3,2,6,5:T(8,128)} fusion(f32[2048,20,512,1,1]{2,0,1,4,3:T(8,128)} %bitcast.7, f32[2048,2,2,128]{0,3,2,1:T(8,128)} %all-gather.11.cloned.1.call-done), kind=kOutput, calls=%fused_computation.12 | convolution fusion | flops 128849018880 | bytes 109051904 | tf_op jit(solution)/shard_map/alc,astb->lcstb/dot_general | solution.py:18
  2666.4 23.5 copy.67
  2689.9 28.9 convolution_bitcast_fusion
  2718.8 46.5 %fusion.31 = f32[512,2,2,512]{0,3,2,1:T(8,128)} fusion(f32[128,20,512]{2,0,1:T(8,128)} %param.6, f32[512,128,20,2,2]{1,2,4,3,0:T(8,128)} %convolution_bitcast_fusion), kind=kOutput, calls=%fused_computation.27 | convolution fusion | flops 32212254720 | bytes 30408704 | tf_op jit(solution)/shard_map/cbruv,brd->cuvd/dot_general | solution.py:20
  2765.3 48.8 %reduce-scatter.11.cloned.1.call-done = f32[512,2,2,128]{0,3,2,1:T(8,128)} async-done(((f32[512,2,2,512]{0,3,2,1:T(8,128)}), f32[512,2,2,128]{0,3,2,1:T(8,128)}) %reduce-scatter.11.cloned.1.call-update) | async-done | bytes 1048592 | tf_op jit(solution)/shard_map/reduce_scatter | solution.py:21
  2814.1 2.1 multiply_reduce_fusion.1
  2816.2 31.9 %psum.70 = f32[]{:T(128)} all-reduce(f32[]{:T(128)} %multiply_reduce_fusion.1), channel_id=1, replica_groups=mesh['right'=4,'left'=4] {'left','right'}, use_global_device_ids=true, to_apply=%region_19.0 | all-reduce | flops 1 | bytes 8 | tf_op jit(solution)/shard_map/psum | solution.py:14
  2848.8 2.1 multiply_reduce_fusion
  2850.9 32.7 %psum.71 = f32[]{:T(128)} all-reduce(f32[]{:T(128)} %get-tuple-element.15), channel_id=1, replica_groups=mesh['right'=4,'left'=4] {'left','right'}, use_global_device_ids=true, to_apply=%region_21.0 | all-reduce | flops 1 | bytes 8 | tf_op jit(solution)/shard_map/psum | solution.py:14
  2884.3 0.1 broadcast_divide_fusion
  2884.4 1.3 copy.51
  2885.7 0.6 pad_maximum_fusion
  2886.3 0.6 pad_maximum_fusion.1
  (19 shorter events, 0.1 us)
Async XLA Ops:
  99.6 18.8 copy-start.1
  99.6 1130.6 %copy-start.2 = (f32[20,20,2,2,2,2]{1,5,4,3,2,0:T(2,128)S(1)}, f32[20,20,2,2,2,2]{1,5,4,3,2,0:T(2,128)}, u32[]{:S(2)}) copy-start(f32[20,20,2,2,2,2]{1,5,4,3,2,0:T(2,128)} %param.7) | copy-start | bytes 76804
  99.6 1130.8 %all-to-all-start = ((f32[512,20,2048]{0,1,2:T(8,128)}), f32[512,20,2048]{0,1,2:T(8,128)}, u32[]{:S(2)}, u32[]{:S(2)}) async-start(f32[512,20,2048]{0,1,2:T(8,128)} %copy.32), calls=%async_computation | async-start | bytes 201326592 | tf_op jit(solution)/shard_map/all_to_all | solution.py:24
  118.4 1202.0 %all-gather.5.cloned.1.call-start = ((), (), s32[]{:S(2)}) async-start(), calls=%async_computation.5 | async-start | bytes 5242880 | tf_op jit(solution)/shard_map/all_gather | solution.py:17
  1230.2 385.8 %reduce-scatter.5.cloned.1.call-start = ((), (), s32[]{:S(2)}) async-start(), calls=%async_computation.6 | async-start | bytes 5242880 | tf_op jit(solution)/shard_map/reduce_scatter | solution.py:21
  1566.3 155.7 %all-gather.7.cloned.1.call-start = ((), (), s32[]{:S(2)}) async-start(), calls=%async_computation.7 | async-start | bytes 5242880 | tf_op jit(solution)/shard_map/all_gather | solution.py:17
  1688.6 328.2 %reduce-scatter.7.cloned.1.call-start = ((), (), s32[]{:S(2)}) async-start(), calls=%async_computation.8 | async-start | bytes 5242880 | tf_op jit(solution)/shard_map/reduce_scatter | solution.py:21
  1921.4 95.4 %copy-start = (f32[512,2,2,128]{0,3,2,1:T(8,128)S(1)}, f32[512,2,2,128]{0,3,2,1:T(8,128)}, u32[]{:S(2)}) copy-start(f32[512,2,2,128]{0,3,2,1:T(8,128)} %broadcast_divide_fusion.3) | copy-start | bytes 3145732
  1968.0 153.5 %all-gather.9.cloned.1.call-start = ((), (), s32[]{:S(2)}) async-start(), calls=%async_computation.9 | async-start | bytes 5242880 | tf_op jit(solution)/shard_map/all_gather | solution.py:17
  2088.1 326.8 %reduce-scatter.9.cloned.1.call-start = ((), (), s32[]{:S(2)}) async-start(), calls=%async_computation.10 | async-start | bytes 5242880 | tf_op jit(solution)/shard_map/reduce_scatter | solution.py:21
  2268.3 52.8 %slice-start = ((s8[5242880]{0:T(1024)(128)(4,1)}), s8[1048576]{0:T(1024)(128)(4,1)S(1)}, s32[]{:S(2)}) async-start(s8[5242880]{0:T(1024)(128)(4,1)} %bitcast.107), calls=%async_computation.13 | async-start | bytes 2097152
  2292.0 29.1 %slice-start.1 = ((s8[5242880]{0:T(1024)(128)(4,1)}), s8[4194304]{0:T(1024)(128)(4,1)S(1)}, s32[]{:S(2)}) async-start(s8[5242880]{0:T(1024)(128)(4,1)} %bitcast.107), calls=%async_computation.14 | async-start | bytes 8388608
  2366.1 153.5 %all-gather.11.cloned.1.call-start = ((), (), s32[]{:S(2)}) async-start(), calls=%async_computation.11 | async-start | bytes 5242880 | tf_op jit(solution)/shard_map/all_gather | solution.py:17
  2486.2 327.9 %reduce-scatter.11.cloned.1.call-start = ((), (), s32[]{:S(2)}) async-start(), calls=%async_computation.12 | async-start | bytes 5242880 | tf_op jit(solution)/shard_map/reduce_scatter | solution.py:21
Sparse Core Ops, SparseCore 0:
  1230.3 33.2 all-gather.4
  1566.5 49.4 reduce-scatter.4
  1688.7 33.2 all-gather.6
  1968.1 48.6 reduce-scatter.6
  2088.2 33.2 all-gather.8
  2366.2 48.6 reduce-scatter.8
  2486.4 33.2 all-gather.10
  2765.5 48.6 reduce-scatter.10
where the time goes:
time: 2900 us; the launch traced here: 2890 us
  blocking collectives  1370 us (47%)
  matrix products  887 us (31%)
  waiting for transfers between devices  296 us (10%)
  local copies, waits for them, and re-layouts  279 us (10%)
    psum x9, blocking collectives, global_dot(): return lax.psum(jnp.sum(vec_one * vec_two), ('left', 'right'))  1370 us
    dot_general x4, matrix products, apply_ham(): jnp.einsum('alc,astb->lcstb', env_cols, gathered, precision=PREC_HIGH, pr...  587 us
    reduce_scatter x4, waiting for transfers between devices, apply_ham(): lax.psum_scatter(partial_out, 'right', scatter_dimension=3, tiled=True)  196 us
    dot_general x4, matrix products, apply_ham(): jnp.einsum('cbruv,brd->cuvd', t_two, env_right, precision=PREC_HIGH, pref...  185 us
    dot_general x4, matrix products, apply_ham(): jnp.einsum('lcstb,lrstuv->cbruv', t_one, mpo_two, precision=PREC_HIGH, pr...  116 us
    all_gather x4, waiting for transfers between devices, apply_ham(): gathered = lax.all_gather(vec_block, 'left', axis=0, tiled=True)  100 us
    unnamed x14, local copies, waits for them, and re-layouts  94.8 us
    dot_general x4, local copies, waits for them, and re-layouts, apply_ham(): jnp.einsum('alc,astb->lcstb', env_cols, gathered, precision=PREC_HIGH, pr...  94.7 us
  transfers between devices with their start and end apart: 9, of which 7 were waited for; matrix products, arithmetic and copies ran while one was open for 3% of the time, Pallas kernels for 0%

commit v1 on v0

--- a/solution.py
+++ b/solution.py
@@ -13,15 +13,15 @@
     def global_dot(vec_one, vec_two):
         return lax.psum(jnp.sum(vec_one * vec_two), ('left', 'right'))
 
-    def apply_ham(vec_block, env_cols, env_right, mpo_two):
-        gathered = lax.all_gather(vec_block, 'left', axis=0, tiled=True)
-        t_one = jnp.einsum('alc,astb->lcstb', env_cols, gathered, precision=PREC_HIGH, preferred_element_type=jnp.float32)
-        t_two = jnp.einsum('lcstb,lrstuv->cbruv', t_one, mpo_two, precision=PREC_HIGH, preferred_element_type=jnp.float32)
-        partial_out = jnp.einsum('cbruv,brd->cuvd', t_two, env_right, precision=PREC_HIGH, preferred_element_type=jnp.float32)
-        return lax.psum_scatter(partial_out, 'right', scatter_dimension=3, tiled=True)
+    def apply_ham(vec_block, left_env, right_cols, mpo_two):
+        gathered = lax.all_gather(vec_block, 'right', axis=3, tiled=True)
+        u_one = jnp.einsum('astb,brd->rstad', gathered, right_cols, precision=PREC_HIGH, preferred_element_type=jnp.float32)
+        u_two = jnp.einsum('rstad,lrstuv->aluvd', u_one, mpo_two, precision=PREC_HIGH, preferred_element_type=jnp.float32)
+        partial_out = jnp.einsum('alc,aluvd->cuvd', left_env, u_two, precision=PREC_HIGH, preferred_element_type=jnp.float32)
+        return lax.psum_scatter(partial_out, 'left', scatter_dimension=0, tiled=True)
 
     def lanczos(psi_block, left_env, right_env, mpo_two):
-        env_cols = lax.all_to_all(left_env, 'left', split_axis=2, concat_axis=0, tiled=True)
+        right_cols = lax.all_to_all(right_env, 'right', split_axis=2, concat_axis=0, tiled=True)
         elem_count = psi_block.size * device_count
         vec_cur = psi_block * jnp.sqrt(elem_count / global_dot(psi_block, psi_block))
         vec_prev = vec_cur
@@ -29,7 +29,7 @@
         alpha_list = []
         beta_list = []
         for step_idx in range(LANCZOS_STEPS):
-            next_vec = apply_ham(vec_cur, env_cols, right_env, mpo_two)
+            next_vec = apply_ham(vec_cur, left_env, right_cols, mpo_two)
             alpha_val = global_dot(vec_cur, next_vec) / elem_count
             next_vec = next_vec - alpha_val * vec_cur
             if step_idx > 0:

time: 2900 us -> 1730 us (0.60)
  blocking collectives: 1370 us -> 398 us
  local copies, waits for them, and re-layouts: 279 us -> 14.3 us
  matrix products: 887 us -> 954 us
    psum x9, blocking collectives: 1370 us -> 293 us  [global_dot(): return lax.psum(jnp.sum(vec_one * vec_two), ('left', 'right'))]
    all_to_all x0 -> x1, blocking collectives: none -> 105 us  [lanczos(): lax.all_to_all(right_env, 'right', split_axis=2, concat_axis=0, tiled=True)]
    dot_general x4 -> x0, local copies, waits for them, and re-layouts: 94.7 us -> none  [apply_ham(): jnp.einsum('alc,astb->lcstb', env_cols, gathered, precision=PREC_HIGH, pr...]
    unnamed x14 -> x8, local copies, waits for them, and re-layouts: 94.8 us -> 8.09 us
    all_to_all x1, local copies, waits for them, and re-layouts: 90 us -> 6.17 us  [lanczos(): lax.all_to_all(right_env, 'right', split_axis=2, concat_axis=0, tiled=True)]
    dot_general x12, matrix products: 887 us -> 954 us  [the longest x4 609 us: apply_ham(): jnp.einsum('alc,aluvd->cuvd', left_env, u_two, precision=PREC_HIGH, prefe...]
    all_gather x4, waiting for transfers between devices: 100 us -> 148 us  [apply_ham(): gathered = lax.all_gather(vec_block, 'right', axis=3, tiled=True)]
    reduce_scatter x4, waiting for transfers between devices: 196 us -> 161 us  [apply_ham(): lax.psum_scatter(partial_out, 'left', scatter_dimension=0, tiled=True)]
  transfers between devices with their start and end apart: 9 -> 8, of which waited for: 7 -> 7; matrix products, arithmetic and copies ran while one was open for 3% -> 1% of each run, Pallas kernels for 0% -> 0%
where the time goes in v1:
time: 1730 us; the launch traced here: 1720 us
  matrix products  954 us (55%)
  blocking collectives  398 us (23%)
  waiting for transfers between devices  309 us (18%)
  other arithmetic  27.7 us (2%)
  between operations  20.8 us (1%)
    dot_general x4, matrix products, apply_ham(): jnp.einsum('alc,aluvd->cuvd', left_env, u_two, precision=PREC_HIGH, prefe...  609 us
    psum x9, blocking collectives, global_dot(): return lax.psum(jnp.sum(vec_one * vec_two), ('left', 'right'))  293 us
    dot_general x4, matrix products, apply_ham(): jnp.einsum('rstad,lrstuv->aluvd', u_one, mpo_two, precision=PREC_HIGH, pr...  198 us
    reduce_scatter x4, waiting for transfers between devices, apply_ham(): lax.psum_scatter(partial_out, 'left', scatter_dimension=0, tiled=True)  161 us
    all_gather x4, waiting for transfers between devices, apply_ham(): gathered = lax.all_gather(vec_block, 'right', axis=3, tiled=True)  148 us
    dot_general x4, matrix products, apply_ham(): jnp.einsum('astb,brd->rstad', gathered, right_cols, precision=PREC_HIGH,...  146 us
    all_to_all x1, blocking collectives, lanczos(): lax.all_to_all(right_env, 'right', split_axis=2, concat_axis=0, tiled=True)  105 us
  transfers between devices with their start and end apart: 8, of which 7 were waited for; matrix products, arithmetic and copies ran while one was open for 1% of the time, Pallas kernels for 0%

profile of v1, /device:TPU:0, one launch (start us, length us, event | category | flops | bytes accessed | tf_op | source)
XLA Modules:
  0.0 1723.5 jit_solution(12366568807782474112)
XLA Ops:
  7.2 0.0 all-gather.5.cloned.1.call-start
  7.2 2.9 multiply_reduce_fusion.8
  10.1 34.7 %psum.63 = f32[]{:T(128)} all-reduce(f32[]{:T(128)} %multiply_reduce_fusion.8), channel_id=1, replica_groups=mesh['right'=4,'left'=4] {'left','right'}, use_global_device_ids=true, to_apply=%region_1.0 | all-reduce | flops 1 | bytes 8 | tf_op jit(solution)/shard_map/psum | solution.py:14
  45.6 2.3 copy_multiply_fusion
  47.8 0.0 all-gather.5.cloned.1.call-update
  47.9 0.0 reduce-scatter.5.cloned.1.call-start
  47.9 6.3 copy.32
  54.2 104.7 %all_to_all.18 = f32[128,20,512]{0,1,2:T(8,128)} all-to-all(f32[128,20,512]{0,1,2:T(8,128)} %copy.32), channel_id=1, replica_groups=mesh['right'=4,'left'=4] {'right'}, dimensions={2} | all-to-all | bytes 10485760 | tf_op jit(solution)/shard_map/all_to_all | solution.py:24
  158.9 6.2 copy.34
  165.1 36.6 %convolution_bitcast_fusion.3 = f32[20,2,2,512,128,1,1]{4,3,0,2,1,6,5:T(8,128)S(1)} fusion(f32[512,20,128,1,1]{2,0,1,4,3:T(8,128)} %bitcast.128, f32[512,2,2,512]{3,0,2,1:T(8,128)} %all-gather.5.cloned.1.call-done), kind=kOutput, calls=%fused_computation.27 | convolution fusion | flops 32212254720 | bytes 30408704 | tf_op jit(solution)/shard_map/astb,brd->rstad/dot_general | solution.py:18
  201.7 49.6 %fusion.20 = f32[512,20,2,2,128]{4,1,3,2,0:T(8,128)} fusion(f32[20,2,2,512,128,1,1]{4,3,0,2,1,6,5:T(8,128)S(1)} %convolution_bitcast_fusion.3, f32[20,20,2,2,2,2]{1,5,4,3,2,0:T(2,128)S(1)} %copy-done.2), kind=kOutput, calls=%fused_computation.20 | convolution fusion | flops 5033164800 | bytes 41968640 | tf_op jit(solution)/shard_map/rstad,lrstuv->aluvd/dot_general | solution.py:19
  251.3 161.6 %fusion.36 = f32[2048,2,2,128]{3,0,2,1:T(8,128)} fusion(f32[512,20,2048]{2,0,1:T(8,128)} %param.5, f32[512,20,2,2,128]{4,1,3,2,0:T(8,128)} %fusion.20), kind=kOutput, calls=%fused_computation.32 | convolution fusion | flops 128849018880 | bytes 109051904 | tf_op jit(solution)/shard_map/alc,aluvd->cuvd/dot_general | solution.py:20
  412.9 0.0 reduce-scatter.5.cloned.1.call-update
  412.9 0.0 all-gather.7.cloned.1.call-start
  413.0 40.2 %reduce-scatter.5.cloned.1.call-done = f32[512,2,2,128]{3,0,2,1:T(8,128)} async-done(((f32[2048,2,2,128]{3,0,2,1:T(8,128)}), f32[512,2,2,128]{3,0,2,1:T(8,128)}) %reduce-scatter.5.cloned.1.call-update) | async-done | bytes 1048592 | tf_op jit(solution)/shard_map/reduce_scatter | solution.py:21
  453.2 2.1 multiply_reduce_fusion.7
  455.3 31.9 %psum.64 = f32[]{:T(128)} all-reduce(f32[]{:T(128)} %multiply_reduce_fusion.7), channel_id=1, replica_groups=mesh['right'=4,'left'=4] {'left','right'}, use_global_device_ids=true, to_apply=%region_4.0 | all-reduce | flops 1 | bytes 8 | tf_op jit(solution)/shard_map/psum | solution.py:14
  487.8 2.1 multiply_reduce_fusion.6
  489.9 32.7 %psum.65 = f32[]{:T(128)} all-reduce(f32[]{:T(128)} %multiply_reduce_fusion.6), channel_id=1, replica_groups=mesh['right'=4,'left'=4] {'left','right'}, use_global_device_ids=true, to_apply=%region_6.0 | all-reduce | flops 1 | bytes 8 | tf_op jit(solution)/shard_map/psum | solution.py:14
  523.3 2.3 broadcast_divide_fusion.3
  525.7 0.0 all-gather.7.cloned.1.call-update
  525.7 0.0 reduce-scatter.7.cloned.1.call-start
  525.7 49.3 %all-gather.7.cloned.1.call-done = f32[512,2,2,512]{3,0,2,1:T(8,128)} async-done(((f32[512,2,2,128]{3,0,2,1:T(8,128)}), f32[512,2,2,512]{3,0,2,1:T(8,128)}) %all-gather.7.cloned.1.call-update) | async-done | bytes 4194320 | tf_op jit(solution)/shard_map/all_gather | solution.py:17
  575.0 36.6 %convolution_bitcast_fusion.2 = f32[20,2,2,512,128,1,1]{4,3,0,2,1,6,5:T(8,128)S(1)} fusion(f32[512,20,128,1,1]{2,0,1,4,3:T(8,128)} %bitcast.129, f32[512,2,2,512]{3,0,2,1:T(8,128)} %all-gather.7.cloned.1.call-done), kind=kOutput, calls=%fused_computation.26 | convolution fusion | flops 32212254720 | bytes 30408704 | tf_op jit(solution)/shard_map/astb,brd->rstad/dot_general | solution.py:18
  611.6 49.5 %fusion.23 = f32[512,20,2,2,128]{4,1,3,2,0:T(8,128)} fusion(f32[20,2,2,512,128,1,1]{4,3,0,2,1,6,5:T(8,128)S(1)} %convolution_bitcast_fusion.2, f32[20,20,2,2,2,2]{1,5,4,3,2,0:T(2,128)S(1)} %copy-done.2), kind=kOutput, calls=%fused_computation.21 | convolution fusion | flops 5033164800 | bytes 41968640 | tf_op jit(solution)/shard_map/rstad,lrstuv->aluvd/dot_general | solution.py:19
  661.1 149.2 %fusion.41 = f32[2048,2,2,128]{3,0,2,1:T(8,128)} fusion(f32[512,20,2048]{2,0,1:T(8,128)} %param.5, f32[512,20,2,2,128]{4,1,3,2,0:T(8,128)} %fusion.23), kind=kOutput, calls=%fused_computation.33 | convolution fusion | flops 128849018880 | bytes 109051904 | tf_op jit(solution)/shard_map/alc,aluvd->cuvd/dot_general | solution.py:20
  810.3 0.0 reduce-scatter.7.cloned.1.call-update
  810.3 0.0 all-gather.9.cloned.1.call-start
  810.4 40.2 %reduce-scatter.7.cloned.1.call-done = f32[512,2,2,128]{3,0,2,1:T(8,128)} async-done(((f32[2048,2,2,128]{3,0,2,1:T(8,128)}), f32[512,2,2,128]{3,0,2,1:T(8,128)}) %reduce-scatter.7.cloned.1.call-update) | async-done | bytes 1048592 | tf_op jit(solution)/shard_map/reduce_scatter | solution.py:21
  850.6 2.1 multiply_reduce_fusion.5
  852.7 31.9 %psum.66 = f32[]{:T(128)} all-reduce(f32[]{:T(128)} %multiply_reduce_fusion.5), channel_id=1, replica_groups=mesh['right'=4,'left'=4] {'left','right'}, use_global_device_ids=true, to_apply=%region_9.0 | all-reduce | flops 1 | bytes 8 | tf_op jit(solution)/shard_map/psum | solution.py:14
  885.2 2.1 multiply_reduce_fusion.4
  887.3 32.7 %psum.67 = f32[]{:T(128)} all-reduce(f32[]{:T(128)} %get-tuple-element.19), channel_id=1, replica_groups=mesh['right'=4,'left'=4] {'left','right'}, use_global_device_ids=true, to_apply=%region_11.0 | all-reduce | flops 1 | bytes 8 | tf_op jit(solution)/shard_map/psum | solution.py:14
  920.8 1.0 broadcast_divide_fusion.2
  921.8 0.0 all-gather.9.cloned.1.call-update
  921.8 0.0 reduce-scatter.9.cloned.1.call-start
  921.9 49.3 %all-gather.9.cloned.1.call-done = f32[512,2,2,512]{3,0,2,1:T(8,128)} async-done(((f32[512,2,2,128]{3,0,2,1:T(8,128)}), f32[512,2,2,512]{3,0,2,1:T(8,128)}) %all-gather.9.cloned.1.call-update) | async-done | bytes 4194320 | tf_op jit(solution)/shard_map/all_gather | solution.py:17
  971.1 36.6 %convolution_bitcast_fusion.1 = f32[20,2,2,512,128,1,1]{4,3,0,2,1,6,5:T(8,128)S(1)} fusion(f32[512,20,128,1,1]{2,0,1,4,3:T(8,128)} %bitcast.130, f32[512,2,2,512]{3,0,2,1:T(8,128)} %all-gather.9.cloned.1.call-done), kind=kOutput, calls=%fused_computation.25 | convolution fusion | flops 32212254720 | bytes 30408704 | tf_op jit(solution)/shard_map/astb,brd->rstad/dot_general | solution.py:18
  1007.7 49.7 %fusion.26 = f32[512,20,2,2,128]{4,1,3,2,0:T(8,128)} fusion(f32[20,2,2,512,128,1,1]{4,3,0,2,1,6,5:T(8,128)S(1)} %convolution_bitcast_fusion.1, f32[20,20,2,2,2,2]{1,5,4,3,2,0:T(2,128)S(1)} %copy-done.2), kind=kOutput, calls=%fused_computation.22 | convolution fusion | flops 5033164800 | bytes 41968640 | tf_op jit(solution)/shard_map/rstad,lrstuv->aluvd/dot_general | solution.py:19
  1057.5 149.2 %fusion.46 = f32[2048,2,2,128]{3,0,2,1:T(8,128)} fusion(f32[512,20,2048]{2,0,1:T(8,128)} %param.5, f32[512,20,2,2,128]{4,1,3,2,0:T(8,128)} %fusion.26), kind=kOutput, calls=%fused_computation.34 | convolution fusion | flops 128849018880 | bytes 109051904 | tf_op jit(solution)/shard_map/alc,aluvd->cuvd/dot_general | solution.py:20
  1206.7 0.0 reduce-scatter.9.cloned.1.call-update
  1206.7 0.0 all-gather.11.cloned.1.call-start
  1206.8 40.2 %reduce-scatter.9.cloned.1.call-done = f32[512,2,2,128]{3,0,2,1:T(8,128)} async-done(((f32[2048,2,2,128]{3,0,2,1:T(8,128)}), f32[512,2,2,128]{3,0,2,1:T(8,128)}) %reduce-scatter.9.cloned.1.call-update) | async-done | bytes 1048592 | tf_op jit(solution)/shard_map/reduce_scatter | solution.py:21
  1247.0 2.1 multiply_reduce_fusion.3
  1249.1 31.9 %psum.68 = f32[]{:T(128)} all-reduce(f32[]{:T(128)} %multiply_reduce_fusion.3), channel_id=1, replica_groups=mesh['right'=4,'left'=4] {'left','right'}, use_global_device_ids=true, to_apply=%region_14.0 | all-reduce | flops 1 | bytes 8 | tf_op jit(solution)/shard_map/psum | solution.py:14
  1281.6 2.1 multiply_reduce_fusion.2
  1283.7 32.7 %psum.69 = f32[]{:T(128)} all-reduce(f32[]{:T(128)} %get-tuple-element.17), channel_id=1, replica_groups=mesh['right'=4,'left'=4] {'left','right'}, use_global_device_ids=true, to_apply=%region_16.0 | all-reduce | flops 1 | bytes 8 | tf_op jit(solution)/shard_map/psum | solution.py:14
  1317.1 1.0 broadcast_divide_fusion.1
  1318.2 0.0 all-gather.11.cloned.1.call-update
  1318.2 0.0 reduce-scatter.11.cloned.1.call-start
  1318.2 49.3 %all-gather.11.cloned.1.call-done = f32[512,2,2,512]{3,0,2,1:T(8,128)} async-done(((f32[512,2,2,128]{3,0,2,1:T(8,128)}), f32[512,2,2,512]{3,0,2,1:T(8,128)}) %all-gather.11.cloned.1.call-update) | async-done | bytes 4194320 | tf_op jit(solution)/shard_map/all_gather | solution.py:17
  1367.5 36.6 %convolution_bitcast_fusion = f32[20,2,2,512,128,1,1]{4,3,0,2,1,6,5:T(8,128)S(1)} fusion(f32[512,20,128,1,1]{2,0,1,4,3:T(8,128)} %bitcast.131, f32[512,2,2,512]{3,0,2,1:T(8,128)} %all-gather.11.cloned.1.call-done), kind=kOutput, calls=%fused_computation.24 | convolution fusion | flops 32212254720 | bytes 30408704 | tf_op jit(solution)/shard_map/astb,brd->rstad/dot_general | solution.py:18
  1404.1 49.5 %fusion.29 = f32[512,20,2,2,128]{4,1,3,2,0:T(8,128)} fusion(f32[20,2,2,512,128,1,1]{4,3,0,2,1,6,5:T(8,128)S(1)} %convolution_bitcast_fusion, f32[20,20,2,2,2,2]{1,5,4,3,2,0:T(2,128)S(1)} %copy-done.2), kind=kOutput, calls=%fused_computation.23 | convolution fusion | flops 5033164800 | bytes 41968640 | tf_op jit(solution)/shard_map/rstad,lrstuv->aluvd/dot_general | solution.py:19
  1453.6 149.1 %fusion.51 = f32[2048,2,2,128]{3,0,2,1:T(8,128)} fusion(f32[512,20,2048]{2,0,1:T(8,128)} %param.5, f32[512,20,2,2,128]{4,1,3,2,0:T(8,128)} %fusion.29), kind=kOutput, calls=%fused_computation.35 | convolution fusion | flops 128849018880 | bytes 109051904 | tf_op jit(solution)/shard_map/alc,aluvd->cuvd/dot_general | solution.py:20
  1602.7 0.0 reduce-scatter.11.cloned.1.call-update
  1602.8 40.2 %reduce-scatter.11.cloned.1.call-done = f32[512,2,2,128]{3,0,2,1:T(8,128)} async-done(((f32[2048,2,2,128]{3,0,2,1:T(8,128)}), f32[512,2,2,128]{3,0,2,1:T(8,128)}) %reduce-scatter.11.cloned.1.call-update) | async-done | bytes 1048592 | tf_op jit(solution)/shard_map/reduce_scatter | solution.py:21
  1643.0 2.1 multiply_reduce_fusion.1
  1645.1 31.9 %psum.70 = f32[]{:T(128)} all-reduce(f32[]{:T(128)} %multiply_reduce_fusion.1), channel_id=1, replica_groups=mesh['right'=4,'left'=4] {'left','right'}, use_global_device_ids=true, to_apply=%region_19.0 | all-reduce | flops 1 | bytes 8 | tf_op jit(solution)/shard_map/psum | solution.py:14
  1677.7 2.1 multiply_reduce_fusion
  1679.8 32.7 %psum.71 = f32[]{:T(128)} all-reduce(f32[]{:T(128)} %get-tuple-element.15), channel_id=1, replica_groups=mesh['right'=4,'left'=4] {'left','right'}, use_global_device_ids=true, to_apply=%region_21.0 | all-reduce | flops 1 | bytes 8 | tf_op jit(solution)/shard_map/psum | solution.py:14
  1713.2 0.1 broadcast_divide_fusion
  1713.3 1.8 copy.51
  1715.0 0.6 pad_maximum_fusion.1
  1715.6 0.6 pad_maximum_fusion
  (7 shorter events, 0.0 us)
Async XLA Ops:
  7.2 158.0 %all-gather.5.cloned.1.call-start = ((), (), s32[]{:S(2)}) async-start(), calls=%async_computation.5 | async-start | bytes 5242880 | tf_op jit(solution)/shard_map/all_gather | solution.py:17
  47.9 405.3 %reduce-scatter.5.cloned.1.call-start = ((), (), s32[]{:S(2)}) async-start(), calls=%async_computation.6 | async-start | bytes 5242880 | tf_op jit(solution)/shard_map/reduce_scatter | solution.py:21
  158.9 42.8 %copy-start.2 = (f32[20,20,2,2,2,2]{1,5,4,3,2,0:T(2,128)S(1)}, f32[20,20,2,2,2,2]{1,5,4,3,2,0:T(2,128)}, u32[]{:S(2)}) copy-start(f32[20,20,2,2,2,2]{1,5,4,3,2,0:T(2,128)} %param.7) | copy-start | bytes 76804
  251.3 201.9 %copy-start = (f32[512,2,2,128]{3,2,1,0:T(2,128)S(1)}, f32[512,2,2,128]{3,2,1,0:T(2,128)}, u32[]{:S(2)}) copy-start(f32[512,2,2,128]{3,2,1,0:T(2,128)} %param.4) | copy-start | bytes 3145732
  412.9 162.1 %all-gather.7.cloned.1.call-start = ((), (), s32[]{:S(2)}) async-start(), calls=%async_computation.7 | async-start | bytes 5242880 | tf_op jit(solution)/shard_map/all_gather | solution.py:17
  525.7 324.9 %reduce-scatter.7.cloned.1.call-start = ((), (), s32[]{:S(2)}) async-start(), calls=%async_computation.8 | async-start | bytes 5242880 | tf_op jit(solution)/shard_map/reduce_scatter | solution.py:21
  661.1 189.5 %copy-start.1 = (f32[512,2,2,128]{3,0,2,1:T(8,128)S(1)}, f32[512,2,2,128]{3,0,2,1:T(8,128)}, u32[]{:S(2)}) copy-start(f32[512,2,2,128]{3,0,2,1:T(8,128)} %broadcast_divide_fusion.3) | copy-start | bytes 3145732
  810.3 160.8 %all-gather.9.cloned.1.call-start = ((), (), s32[]{:S(2)}) async-start(), calls=%async_computation.9 | async-start | bytes 5242880 | tf_op jit(solution)/shard_map/all_gather | solution.py:17
  921.8 325.1 %reduce-scatter.9.cloned.1.call-start = ((), (), s32[]{:S(2)}) async-start(), calls=%async_computation.10 | async-start | bytes 5242880 | tf_op jit(solution)/shard_map/reduce_scatter | solution.py:21
  1206.7 160.8 %all-gather.11.cloned.1.call-start = ((), (), s32[]{:S(2)}) async-start(), calls=%async_computation.11 | async-start | bytes 5242880 | tf_op jit(solution)/shard_map/all_gather | solution.py:17
  1318.2 324.8 %reduce-scatter.11.cloned.1.call-start = ((), (), s32[]{:S(2)}) async-start(), calls=%async_computation.12 | async-start | bytes 5242880 | tf_op jit(solution)/shard_map/reduce_scatter | solution.py:21
Sparse Core Ops, SparseCore 0:
  48.0 107.5 all-gather.4
  413.1 40.0 reduce-scatter.4
  525.8 49.1 all-gather.6
  810.5 40.0 reduce-scatter.6
  921.9 49.1 all-gather.8
  1206.8 40.0 reduce-scatter.8
  1318.3 49.1 all-gather.10
  1602.9 40.0 reduce-scatter.10

commit v2 on v1

v2 whole, which is shorter than its diff:
```python
import functools

import jax
import jax.numpy as jnp
from jax import lax
from jax.experimental import pallas as pl
from jax.experimental.pallas import tpu as pltpu
from jax.sharding import PartitionSpec as P

STEPS = 4
W = 20
S = 4
BF = jnp.bfloat16
F32 = jnp.float32
VM_LIMIT = 67043328


class Cfg:
    def __init__(self, lt=256, bl=128, row_chunk=128):
        self.lt = lt
        self.a = 2 * lt
        self.bl = bl
        self.nb = 4 * bl
        self.kb = self.nb // 2
        self.groups = bl // 16
        self.rows = 4 * bl
        self.rc = row_chunk
        self.nl = max(lt // 128, 1)
        self.elems = float(4 * self.a * S * self.nb)


def split3(x):
    one = x.astype(BF)
    rest = x - one.astype(F32)
    two = rest.astype(BF)
    return one, two, (rest - two.astype(F32)).astype(BF)


def remote(src, dst, send_sem, recv_sem, right, left):
    return pltpu.make_async_remote_copy(
        src_ref=src, dst_ref=dst, send_sem=send_sem, recv_sem=recv_sem,
        device_id={'right': right, 'left': left}, device_id_type=pl.DeviceIdType.MESH)


def enter(me):
    barrier = pltpu.get_barrier_semaphore()

    @pl.loop(1, 16)
    def _(off):
        peer = lax.rem(me + off, 16)
        pl.semaphore_signal(barrier, 1, device_id={'right': peer // 4, 'left': lax.rem(peer, 4)},
                            device_id_type=pl.DeviceIdType.MESH)

    pl.semaphore_wait(barrier, 15)


def all_sum(part, k, me, out_ref, in_ref, send_sem, recv_sem):
    out_ref[k] = part
    in_ref[k, me] = part

    def copy(peer, slot):
        return remote(out_ref.at[k], in_ref.at[k, slot], send_sem.at[k, peer], recv_sem.at[k, slot],
                      peer // 4, lax.rem(peer, 4))

    @pl.loop(1, 16)
    def _(off):
        copy(lax.rem(me + off, 16), me).start()

    @pl.loop(1, 16)
    def _(off):
        peer = lax.rem(me + off, 16)
        copy(peer, peer).wait_recv()

    total = in_ref[k, 0]
    for i in range(1, 16):
        total = total + in_ref[k, i]

    @pl.loop(1, 16)
    def _(off):
        copy(lax.rem(me + off, 16), me).wait_send()

    return jnp.sum(jnp.sum(total, axis=1, keepdims=True), axis=0, keepdims=True)


def fold(x):
    r, c = x.shape
    if c % 128 == 0:
        x = jnp.sum(x.reshape(r // 8, 8, c), axis=0)
        acc = x[:, :128]
        for i in range(1, c // 128):
            acc = acc + x[:, i * 128:(i + 1) * 128]
        return acc
    return jnp.full((8, 128), jnp.sum(x) / 1024.0, F32)


def prep_kernel(cfg, l3, rb3, psi, ls, rtf, qg0, nrm,
                ibuf, obuf, rbv, rst, ars, arr,
                isem, osem, lsem, ar_s, ar_r, ps_s, ps_r, rh_s, rh_r, ro_s, ro_r, rf_s, rf_r):
    me_r = lax.axis_index('right')
    me_l = lax.axis_index('left')
    me = me_r * 4 + me_l
    core = lax.rem(me_l, 2)
    mate = me_l + 1 - 2 * core
    bl, lt, rc = cfg.bl, cfg.lt, cfg.rc
    half = W // 2
    nchunk = cfg.a // rc
    total = W * nchunk

    load_r = pltpu.make_async_copy(rb3, rbv, lsem.at[0])
    load_r.start()

    def get(n, slot):
        return pltpu.make_async_copy(l3.at[n // nchunk, pl.ds(pl.multiple_of(lax.rem(n, nchunk) * rc, rc), rc), :],
                                     ibuf.at[slot], isem.at[slot])

    def put(n, slot):
        return pltpu.make_async_copy(
            obuf.at[slot],
            ls.at[:, :, n // nchunk, :, pl.ds(pl.multiple_of(lax.rem(n, nchunk) * rc, rc), rc), :], osem.at[slot])

    get(0, 0).start()
    get(1, 1).start()
    enter(me)

    def psi_copy(off):
        peer = lax.rem(me_r + off, 4)
        return remote(psi, qg0.at[:, :, pl.ds(pl.multiple_of(me_r * bl, bl), bl), :], ps_s.at[off], ps_r.at[me_r], peer, me_l)

    def psi_from(off):
        peer = lax.rem(me_r + off, 4)
        return remote(psi, qg0.at[:, :, pl.ds(pl.multiple_of(peer * bl, bl), bl), :], ps_s.at[off], ps_r.at[peer], peer, me_l)

    def r_half(off):
        peer = lax.rem(me_r + off, 4)
        return remote(rst.at[peer, pl.ds(core * half, half)],
                      rtf.at[pl.ds(core * half, half), :, pl.ds(pl.multiple_of(me_r * bl, bl), bl)],
                      rh_s.at[off], rh_r.at[me_r], peer, me_l)

    def r_from(off):
        peer = lax.rem(me_r + off, 4)
        return remote(rst.at[peer, pl.ds(core * half, half)],
                      rtf.at[pl.ds(core * half, half), :, pl.ds(pl.multiple_of(peer * bl, bl), bl)],
                      rh_s.at[off], rh_r.at[peer], peer, me_l)

    def r_fwd(off, mine):
        peer = lax.rem(me_r + off, 4)
        where = core if mine else 1 - core
        part = rtf.at[pl.ds(where * half, half), :, pl.ds(pl.multiple_of(peer * bl, bl), bl)]
        return remote(part, part, rf_s.at[off], rf_r.at[off], me_r, mate)

    def r_own():
        return remote(rst.at[me_r], rtf.at[:, :, pl.ds(pl.multiple_of(me_r * bl, bl), bl)], ro_s.at[0], ro_r.at[0], me_r, mate)

    own_psi = pltpu.make_async_copy(psi, qg0.at[:, :, pl.ds(pl.multiple_of(me_r * bl, bl), bl), :], lsem.at[1])
    own_psi.start()

    load_r.wait()
    for j in range(4):
        @pl.loop(0, W)
        def _(r):
            rst[j, r] = rbv[r, :, j * bl:(j + 1) * bl].T
    for off in range(1, 4):
        r_half(off).start()
    r_own().start()
    for off in range(1, 4):
        psi_copy(off).start()

    part = jnp.zeros((8, 128), F32)
    for h in range(2):
        for s in range(S):
            x = psi[h, s]
            part = part + fold(x * x)
    tot = all_sum(part, 0, me, ars, arr, ar_s, ar_r)
    nrm[...] = jnp.broadcast_to(tot, (8, 128))

    forward_at = (total // 4) * 3

    @pl.loop(0, total)
    def _(n):
        slot = lax.rem(n, 2)

        @pl.when(n == forward_at)
        def _():
            for off in range(1, 4):
                r_from(off).wait_recv()
            for off in range(1, 4):
                r_fwd(off, True).start()

        get(n, slot).wait()

        @pl.when(n >= 2)
        def _():
            put(n - 2, slot).wait()

        for d in range(4):
            for h in range(2):
                c0 = (2 * d + h) * lt
                for k, v in enumerate(split3(ibuf[slot, :, c0:c0 + lt])):
                    obuf[slot, d, h, k] = v

        put(n, slot).start()

        @pl.when(n + 2 < total)
        def _():
            get(n + 2, slot).start()

    put(total - 2, total % 2).wait()
    put(total - 1, (total - 1) % 2).wait()
    own_psi.wait()
    for off in range(1, 4):
        psi_from(off).wait_recv()
        psi_copy(off).wait_send()
        r_half(off).wait_send()
        r_fwd(off, False).wait_recv()
        r_fwd(off, True).wait_send()
    r_own().wait_recv()
    r_own().wait_send()


def prep(cfg, l3, rb3, psi):
    a, bl, nb, lt = cfg.a, cfg.bl, cfg.nb, cfg.lt
    hbm = pl.BlockSpec(memory_space=pl.ANY)
    vm = pl.BlockSpec(memory_space=pltpu.VMEM)
    dma = pltpu.SemaphoreType.DMA
    return pl.pallas_call(
        functools.partial(prep_kernel, cfg),
        out_shape=(
            jax.ShapeDtypeStruct((4, 2, W, 3, a, lt), BF),
            jax.ShapeDtypeStruct((W, bl, nb), F32),
            jax.ShapeDtypeStruct((2, S, nb, lt), F32),
            jax.ShapeDtypeStruct((8, 128), F32),
        ),
        in_specs=[hbm, hbm, vm],
        out_specs=(hbm, hbm, hbm, vm),
        scratch_shapes=[
            pltpu.VMEM((2, cfg.rc, 4 * a), F32),
            pltpu.VMEM((2, 4, 2, 3, cfg.rc, lt), BF),
            pltpu.VMEM((W, bl, nb), F32),
            pltpu.VMEM((4, W, bl, bl), F32),
            pltpu.VMEM((1, 8, 128), F32),
            pltpu.VMEM((1, 16, 8, 128), F32),
            dma((2,)), dma((2,)), dma((2,)), dma((1, 16)), dma((1, 16)),
            dma((4,)), dma((4,)), dma((4,)), dma((4,)), dma((1,)), dma((1,)), dma((4,)), dma((4,)),
        ],
        compiler_params=pltpu.CompilerParams(collective_id=0, has_side_effects=True, vmem_limit_bytes=VM_LIMIT),
    )(l3, rb3, psi)


NL = 4


def steps_kernel(cfg, ls, rtf, qg0, wl, nrm, out_v, out_s,
                 u2, rts, vg, qg, lb, sb, rb0, yb, xs, ub0, ub1, ob, vp, acc, rcb, cf, al, ars, arr,
                 lsem, rcsem, qsem, ar_s, ar_r, rs_s, rs_r, ag_s, ag_r, credit):
    lt, bl, nb, kb, rows, groups = cfg.lt, cfg.bl, cfg.nb, cfg.kb, cfg.rows, cfg.groups
    nl, lw = cfg.nl, cfg.lt // cfg.nl
    me_r = lax.axis_index('right')
    me_l = lax.axis_index('left')
    me = me_r * 4 + me_l
    core = lax.rem(me_l, 2)
    chip = me_l // 2
    mate = chip * 2 + 1 - core
    across = (1 - chip) * 2 + core
    own = pl.ds(pl.multiple_of(me_r * bl, bl), bl)
    trips = W // NL
    low = lax.broadcasted_iota(jnp.int32, (8, lt), 0) < 4

    load_q = pltpu.make_async_copy(qg0, qg, qsem)
    load_q.start()

    def get_r(i, slot):
        return pltpu.make_async_copy(rtf.at[:, pl.ds(pl.multiple_of(i * 8, 8), 8), :], rcb.at[slot], rcsem.at[slot])

    get_r(0, 0).start()
    enter(me)
    vg[...] = jnp.zeros(vg.shape, F32)
    ub1[...] = jnp.zeros(ub1.shape, F32)
    lowb = lax.broadcasted_iota(jnp.int32, (8, nb), 0) < 4

    @pl.loop(0, bl // 8)
    def _(i):
        slot = lax.rem(i, 2)

        @pl.when(i + 1 < bl // 8)
        def _():
            get_r(i + 1, 1 - slot).start()

        get_r(i, slot).wait()
        one = jnp.transpose(rcb[slot, 0:8], (1, 0, 2))
        two = jnp.transpose(rcb[slot, 8:16], (1, 0, 2))
        tail = rcb[slot, 16:20]
        tail = jnp.transpose(jnp.concatenate([tail, tail], axis=0), (1, 0, 2))
        for quad in range(2):
            b0 = 4 * quad
            parts = []
            for b in range(b0, b0 + 4):
                parts += [one[b], two[b]]
            parts += [jnp.where(lowb, tail[b0], tail[b0 + 1]), jnp.where(lowb, tail[b0 + 2], tail[b0 + 3])]
            for k, v in enumerate(split3(jnp.concatenate(parts, axis=0))):
                rts[k, pl.ds(pl.multiple_of(i * 160 + 80 * quad, 16), 80), :] = v

    norm = jnp.sqrt(nrm[...] / cfg.elems)
    cf[0] = jnp.zeros((8, 128), F32)
    cf[1] = 1.0 / norm
    cf[2] = norm
    load_q.wait()

    def place(n):
        h = n // (4 * trips)
        who = lax.rem(n // trips, 4)
        to = lax.rem(chip + 1 - who // 2, 2) * 2 + lax.rem(core + 1 - lax.rem(who, 2), 2)
        return to, h, lax.rem(n, trips)

    def get_l(n):
        d, h, p = place(n)
        slot = lax.rem(n + 1, 2)
        return pltpu.make_async_copy(ls.at[d, h, pl.ds(p * NL, NL)], lb.at[slot, :, :, :cfg.a], lsem.at[slot])

    def ag_copy(h, off):
        peer = lax.rem(me_r + off, 4)
        return remote(qg.at[h, :, own, :], qg.at[h, :, own, :], ag_s.at[h, off], ag_r.at[h, me_r], peer, me_l)

    def ag_from(h, off):
        peer = lax.rem(me_r + off, 4)
        there = qg.at[h, :, pl.ds(pl.multiple_of(peer * bl, bl), bl), :]
        return remote(there, there, ag_s.at[h, off], ag_r.at[h, peer], peer, me_l)

    def coef(i, shape):
        one = cf[i, 0:1, 0:1]
        return jnp.broadcast_to(one, shape)

    def update(h, j):
        @pl.when(j > 0)
        def _():
            for off in range(1, 4):
                ag_from(h, off).wait_recv()
                ag_copy(h, off).wait_send()

        for s in range(S):
            vp[h, s] = vg[h, s, own, :]
        chunk = min(64, nb)

        @pl.loop(0, S * (nb // chunk))
        def _(i):
            s = i // (nb // chunk)
            at = pl.ds(pl.multiple_of(lax.rem(i, nb // chunk) * chunk, chunk), chunk)
            new = (qg[h, s, at, :] - coef(0, (chunk, lt)) * vg[h, s, at, :]) * coef(1, (chunk, lt))
            vg[h, s, at, :] = new
            for k, v in enumerate(split3(new)):
                lb[0, s, k, at, :] = v

        @pl.when(j < STEPS - 1)
        def _():
            for off in range(1, 4):
                pl.semaphore_signal(credit.at[h], 1, device_id={'right': lax.rem(me_r + off, 4), 'left': me_l},
                                    device_id_type=pl.DeviceIdType.MESH)

    def w_tile(ub, quad, i):
        base = 80 * quad
        pair = base + 64 + 8 * (i // 2)
        parts = [ub[s, base + 16 * i:base + 16 * i + 16, :] for s in range(S)]
        for s in (0, 2):
            one, two = ub[s, pair:pair + 8, :], ub[s + 1, pair:pair + 8, :]
            if i % 2 == 0:
                parts.append(jnp.where(low, one, pltpu.roll(two, 4, 0)))
            else:
                parts.append(jnp.where(low, pltpu.roll(one, 4, 0), two))
        x = jnp.concatenate(parts, axis=0)
        return jnp.concatenate([*split3(x), jnp.zeros((16, lt), BF)], axis=0)

    def w_finish(quad, g, h):
        even, odd = [], []
        for i in range(W // 2):
            v = [ob[b, 8 * i:8 * i + 8, :] for b in range(4)]
            for dst, b0 in ((even, 0), (even, 2)):
                dst.append(jnp.where(low, v[b0], pltpu.roll(v[b0 + 1], 4, 0)))
            for dst, b0 in ((odd, 0), (odd, 2)):
                dst.append(jnp.where(low, pltpu.roll(v[b0], 4, 0), v[b0 + 1]))
        at = pl.ds(pl.multiple_of(g * 64 + 16 * quad, 16), 16)
        col = pl.ds(pl.multiple_of(h * lt, lt), lt)
        for first, lst in ((0, even), (1, odd)):
            for k, v in enumerate(split3(jnp.concatenate(lst, axis=0))):
                for i in range(W // 2):
                    u2[2 * i + first, k, at, col] = v[16 * i:16 * i + 16]

    def group(it, ub_new, ub_old, do_r=True):
        before = lax.rem(it + 2 * groups - 1, 2 * groups)
        gw, hw = lax.rem(before, groups), before // groups
        at = pl.ds(pl.multiple_of(lax.rem(it, groups) * (16 * W), 16 * W), 16 * W)
        for s in range(S):
            if do_r:
                total = None
                for k in range(3):
                    for i in range(3 - k):
                        term = jnp.dot(rts[i, at, :], lb[0, s, k, :nb, :], preferred_element_type=F32)
                        total = term if total is None else total + term
                ub_new[s] = total
            for i in range(4):
                y = jnp.dot(wl[...], w_tile(ub_old, s, i), preferred_element_type=F32)
                ob[i] = (y[:4 * W] + y[4 * W:8 * W]) + y[8 * W:]
            w_finish(s, gw, hw)

    def l_trip(n, p):
        get_l(n).wait()

        @pl.when(n + 1 < 8 * trips)
        def _():
            get_l(n + 1).start()

        slot = lax.rem(n + 1, 2)
        total = None
        for m in range(NL):
            for k in range(3):
                for i in range(3 - k):
                    term = jnp.dot(u2[p * NL + m, i], lb[slot, m, k, :cfg.a, :], preferred_element_type=F32)
                    total = term if total is None else total + term
        acc[...] += total

    def rs_copy(k, h):
        dst = (rb0, xs.at[h], yb)[k]
        i = 1 + h if k == 1 else (0 if k == 0 else 3)
        return remote(sb.at[k], dst, rs_s.at[k], rs_r.at[i], me_r, across if k == 1 else mate)

    def l_phase(h, j):
        for who in range(4):
            acc[...] = jnp.zeros((rows, lt), F32)

            @pl.loop(0, trips)
            def _(p):
                l_trip((h * 4 + who) * trips + p, p)

            if who == 1:
                rs_copy(0, h).wait_recv()
            if who == 2:
                rs_copy(0, h).wait_send()
            if who == 3:
                rs_copy(2, h).wait_recv()
                rs_copy(1, h).wait_recv()
            for i in range(nl):
                y = acc[:, i * lw:(i + 1) * lw]
                if who == 1:
                    y = y + rb0[i]
                if who < 3:
                    sb[who, i] = y
                else:
                    yb[i] = (y + yb[i]) + xs[h, i]
            if who < 3:
                rs_copy(who, h).start()

        rs_copy(1, h).wait_send()
        rs_copy(2, h).wait_send()
        beta = coef(2, (bl, lt))
        for t in range(S):
            w = jnp.concatenate([yb[i, pl.ds(t, bl, stride=4), :] for i in range(nl)], axis=1)
            al[...] += fold(w * vg[h, t, own, :])
            qg[h, t, own, :] = w - beta * vp[h, t]

        @pl.when(j < STEPS - 1)
        def _():
            pl.semaphore_wait(credit.at[h], 3)
            for off in range(1, 4):
                ag_copy(h, off).start()

    @pl.loop(0, STEPS)
    def _(j):
        get_l(0).start()

        @pl.loop(0, groups)
        def _(p):
            @pl.when(lax.rem(p, groups // 2) == 0)
            def _():
                update(p // (groups // 2), j)

            group(2 * p, ub0, ub1)
            group(2 * p + 1, ub1, ub0)

        group(2 * groups, ub0, ub1, do_r=False)
        al[...] = jnp.zeros((8, 128), F32)

        @pl.loop(0, 2)
        def _(h):
            l_phase(h, j)

        alpha = jnp.broadcast_to(all_sum(al[...], 0, me, ars, arr, ar_s, ar_r), (8, 128)) / cfg.elems
        cf[0] = alpha
        out_s[j] = alpha
        part = jnp.zeros((8, 128), F32)
        for h in range(2):
            for s in range(S):
                w = qg[h, s, own, :] - coef(0, (bl, lt)) * vg[h, s, own, :]
                part = part + fold(w * w)
        beta = jnp.sqrt(jnp.broadcast_to(all_sum(part, 1, me, ars, arr, ar_s, ar_r), (8, 128)) / cfg.elems)
        cf[1] = 1.0 / beta
        cf[2] = beta
        out_s[STEPS + j] = beta

    for h in range(2):
        for s in range(S):
            out_v[h, s] = (qg[h, s, own, :] - coef(0, (bl, lt)) * vg[h, s, own, :]) * coef(1, (bl, lt))


def steps(cfg, ls, rtf, qg0, wl, nrm):
    lt, bl, nb, rows = cfg.lt, cfg.bl, cfg.nb, cfg.rows
    hbm = pl.BlockSpec(memory_space=pl.ANY)
    vm = pl.BlockSpec(memory_space=pltpu.VMEM)
    dma = pltpu.SemaphoreType.DMA
    block = (cfg.nl, rows, lt // cfg.nl)
    scratch = [
        pltpu.VMEM((W, 3, rows, cfg.a), BF),
        pltpu.VMEM((3, W * bl, nb), BF),
        pltpu.VMEM((2, S, nb, lt), F32),
        pltpu.VMEM((2, S, nb, lt), F32),
        pltpu.VMEM((2, NL, 3, max(cfg.a, nb), lt), BF),
        pltpu.VMEM((3, *block), F32),
        pltpu.VMEM(block, F32),
        pltpu.VMEM(block, F32),
        pltpu.VMEM((2, *block), F32),
        pltpu.VMEM((S, 16 * W, lt), F32),
        pltpu.VMEM((S, 16 * W, lt), F32),
        pltpu.VMEM((4, 4 * W, lt), F32),
        pltpu.VMEM((2, S, bl, lt), F32),
        pltpu.VMEM((rows, lt), F32),
        pltpu.VMEM((2, W, 8, nb), F32),
        pltpu.VMEM((3, 8, 128), F32),
        pltpu.VMEM((8, 128), F32),
        pltpu.VMEM((2, 8, 128), F32),
        pltpu.VMEM((2, 16, 8, 128), F32),
        dma((2,)), dma((2,)), dma, dma((2, 16)), dma((2, 16)), dma((3,)), dma((4,)), dma((2, 4)), dma((2, 4)),
        pltpu.SemaphoreType.REGULAR((2,)),
    ]
    return pl.pallas_call(
        functools.partial(steps_kernel, cfg),
        out_shape=(
            jax.ShapeDtypeStruct((2, S, bl, lt), F32),
            jax.ShapeDtypeStruct((2 * STEPS, 8, 128), F32),
        ),
        in_specs=[hbm, hbm, hbm, vm, vm],
        out_specs=(vm, vm),
        scratch_shapes=scratch,
        compiler_params=pltpu.CompilerParams(collective_id=1, has_side_effects=True, vmem_limit_bytes=VM_LIMIT),
    )(ls, rtf, qg0, wl, nrm)


def mpo_rows(mpo_two):
    w = mpo_two.reshape(W, W, S, S).transpose(0, 3, 2, 1)
    w = jnp.concatenate([w[..., :16].reshape(W * S, 64), w[..., 16:].reshape(W * S, 16)], axis=1)
    one = lax.reduce_precision(w, 8, 7)
    two = lax.reduce_precision(w - one, 8, 7)
    three = w - one - two
    none = jnp.zeros_like(w)
    left = jnp.concatenate([
        jnp.concatenate([one, one, one], 1),
        jnp.concatenate([two, two, none], 1),
        jnp.concatenate([three, none, none], 1)], 0)
    return jnp.pad(left, ((0, 0), (0, 16))).astype(BF)


def build(mesh, cfg):
    def lanczos(psi_block, left_env, right_env, mpo_two):
        lt, a, bl = cfg.lt, cfg.a, cfg.bl
        l3 = jnp.transpose(left_env, (1, 0, 2))
        rb3 = jnp.transpose(right_env, (1, 0, 2))
        psi = psi_block.reshape(2, lt, S, bl).transpose(0, 2, 3, 1)
        wl = mpo_rows(mpo_two)
        ls, rtf, qg0, nrm = prep(cfg, l3, rb3, psi)
        vec, scal = steps(cfg, ls, rtf, qg0, wl, nrm)
        vec = vec.transpose(0, 3, 1, 2).reshape(psi_block.shape)
        return scal[:STEPS, 0, 0], scal[STEPS:, 0, 0], vec

    return jax.shard_map(
        lanczos,
        mesh=mesh,
        in_specs=(P('left', None, None, 'right'), P('left', None, None), P('right', None, None), P()),
        out_specs=(P(), P(), P('left', None, None, 'right')),
        check_vma=False,
    )


def solution(mesh):
    return build(mesh, Cfg())
```

time: 1730 us -> 1060 us (0.61)
  Pallas kernels: 0 us -> 1040 us
  matrix products: 954 us -> 0 us
  blocking collectives: 398 us -> 0 us
  waiting for transfers between devices: 309 us -> 0 us
  other arithmetic: 27.7 us -> 0.2 us
  between operations: 20.8 us -> 0.72 us
    pallas_call x0 -> x2, Pallas kernels: none -> 1040 us  [the longest x1 861 us: steps(): pl.pallas_call(functools.partial(steps_kernel, cfg), out_shape=(jax.Shape...]
    dot_general x12 -> x0, matrix products: 954 us -> none  [the longest x4 609 us: apply_ham(): jnp.einsum('alc,aluvd->cuvd', left_env, u_two, precision=PREC_HIGH, prefe...]
    psum x9 -> x0, blocking collectives: 293 us -> none  [global_dot(): return lax.psum(jnp.sum(vec_one * vec_two), ('left', 'right'))]
    reduce_scatter x4 -> x0, waiting for transfers between devices: 161 us -> none  [apply_ham(): lax.psum_scatter(partial_out, 'left', scatter_dimension=0, tiled=True)]
    all_gather x4 -> x0, waiting for transfers between devices: 148 us -> none  [apply_ham(): gathered = lax.all_gather(vec_block, 'right', axis=3, tiled=True)]
    all_to_all x1 -> x0, blocking collectives: 105 us -> none  [lanczos(): lax.all_to_all(right_env, 'right', split_axis=2, concat_axis=0, tiled=True)]
    reduce_sum x9 -> x0, other arithmetic: 19.7 us -> none  [global_dot(): return lax.psum(jnp.sum(vec_one * vec_two), ('left', 'right'))]
  transfers between devices with their start and end apart: 8 -> 0, of which waited for: 7 -> 0; matrix products, arithmetic and copies ran while one was open for 1% -> 0% of each run, Pallas kernels for 0% -> 0%
where the time goes in v2:
time: 1060 us; the launch traced here: 1050 us
  Pallas kernels  1040 us (98%)
    pallas_call x1, Pallas kernels, steps(): pl.pallas_call(functools.partial(steps_kernel, cfg), out_shape=(jax.Shape...  861 us
    pallas_call x1, Pallas kernels, prep(): pl.pallas_call(functools.partial(prep_kernel, cfg), out_shape=(jax.ShapeD...  184 us

profile of v2, /device:TPU:0, one launch (start us, length us, event | category | flops | bytes accessed | tf_op | source)
XLA Modules:
  0.0 1054.6 jit_solution(7999396258665095453)
XLA Ops:
  0.6 0.0 copy-start
  0.6 1.7 copy.10
  2.4 0.1 slice.16
  2.4 0.2 reshape.26
  2.7 0.1 reshape.24
  2.8 0.1 copy.17
  2.8 0.1 copy.12
  2.9 0.1 reduce-precision_convert_fusion.1
  3.0 0.1 fusion.1
  3.2 0.7 pad.7.wl
  3.8 0.0 copy-done
  3.8 1.3 copy.9
  5.2 183.6 %shard_map.67 = (bf16[4,2,20,3,512,256]{5,4,3,2,1,0:T(8,128)(2,1)}, f32[20,128,512]{2,1,0:T(8,128)}, f32[2,4,512,256]{3,2,1,0:T(8,128)}, f32[8,128]{1,0:T(8,128)}) custom-call(f32[20,512,2048]{2,1,0:T(8,128)} %bitcast.l3, f32[20,128,512]{2,1,0:T(8,128)} %bitcast.12, f32[2,4,128,256]{3,2,1,0:T(8,128)} %bitcast.13), custom_call_target="tpu_custom_call" | custom-call | tf_op jit(solution)/shard_map/pallas_call | solution.py:225
  188.7 861.2 %shard_map.68 = (f32[2,4,128,256]{3,2,1,0:T(8,128)}, f32[8,8,128]{2,1,0:T(8,128)}) custom-call(bf16[4,2,20,3,512,256]{5,4,3,2,1,0:T(8,128)(2,1)} %get-tuple-element.9.ls, f32[20,128,512]{2,1,0:T(8,128)} %get-tuple-element.10.rtf, f32[2,4,512,256]{3,2,1,0:T(8,128)} %get-tuple-element.11.qg0, bf16[240,256]{1,0:T(8,128)(2,1)} %pad.7.wl, ...), custom_call_target="tpu_custom_call" | custom-call | tf_op jit(solution)/shard_map/pallas_call | solution.py:531
  1049.9 1.4 slice_reduce_fusion
  1051.3 1.6 copy.13
  1052.8 1.8 copy.14
  (2 shorter events, 0.0 us)
Async XLA Ops:
  0.6 3.2 copy-start

commit v3 on v2

v3 whole, which is shorter than its diff:
```python
import functools

import jax
import jax.numpy as jnp
from jax import lax
from jax.experimental import pallas as pl
from jax.experimental.pallas import tpu as pltpu
from jax.sharding import PartitionSpec as P

STEPS = 4
W = 20
S = 4
BF = jnp.bfloat16
F32 = jnp.float32
VM_LIMIT = 67043328


class Cfg:
    def __init__(self, lt=256, bl=128):
        self.lt = lt
        self.a = 2 * lt
        self.bl = bl
        self.nb = 4 * bl
        self.kb = self.nb // 2
        self.groups = bl // 16
        self.rows = 4 * bl
        self.nl = max(lt // 128, 1)
        self.elems = float(4 * self.a * S * self.nb)


def split3(x):
    one = x.astype(BF)
    rest = x - one.astype(F32)
    two = rest.astype(BF)
    return one, two, (rest - two.astype(F32)).astype(BF)


def remote(src, dst, send_sem, recv_sem, right, left):
    return pltpu.make_async_remote_copy(
        src_ref=src, dst_ref=dst, send_sem=send_sem, recv_sem=recv_sem,
        device_id={'right': right, 'left': left}, device_id_type=pl.DeviceIdType.MESH)


def enter(me):
    barrier = pltpu.get_barrier_semaphore()

    @pl.loop(1, 16)
    def _(off):
        peer = lax.rem(me + off, 16)
        pl.semaphore_signal(barrier, 1, device_id={'right': peer // 4, 'left': lax.rem(peer, 4)},
                            device_id_type=pl.DeviceIdType.MESH)

    pl.semaphore_wait(barrier, 15)


def all_sum(part, k, me, out_ref, in_ref, send_sem, recv_sem):
    out_ref[k] = part
    in_ref[k, me] = part

    def copy(peer, slot):
        return remote(out_ref.at[k], in_ref.at[k, slot], send_sem.at[k, peer], recv_sem.at[k, slot],
                      peer // 4, lax.rem(peer, 4))

    @pl.loop(1, 16)
    def _(off):
        copy(lax.rem(me + off, 16), me).start()

    @pl.loop(1, 16)
    def _(off):
        peer = lax.rem(me + off, 16)
        copy(peer, peer).wait_recv()

    total = in_ref[k, 0]
    for i in range(1, 16):
        total = total + in_ref[k, i]

    @pl.loop(1, 16)
    def _(off):
        copy(lax.rem(me + off, 16), me).wait_send()

    return jnp.sum(jnp.sum(total, axis=1, keepdims=True), axis=0, keepdims=True)


def fold(x):
    r, c = x.shape
    if c % 128 == 0:
        x = jnp.sum(x.reshape(r // 8, 8, c), axis=0)
        acc = x[:, :128]
        for i in range(1, c // 128):
            acc = acc + x[:, i * 128:(i + 1) * 128]
        return acc
    return jnp.full((8, 128), jnp.sum(x) / 1024.0, F32)


CH = 5


def kernel(cfg, l3, rbt, psi, wl, out_v, out_s, rtf,
           u2, rts, vgs, vg, qg, lb, sb, rb0, yb, xs, ub0, ub1, ob, vp, acc, rcb, cf, al, ars, arr,
           lsem, rcsem, qsem, ar_s, ar_r, rs_s, rs_r, ag_s, ag_r, rh_s, rh_r, ro_s, ro_r, rf_s, rf_r, credit):
    lt, bl, nb, kb, rows, groups = cfg.lt, cfg.bl, cfg.nb, cfg.kb, cfg.rows, cfg.groups
    nl, lw = cfg.nl, cfg.lt // cfg.nl
    me_r = lax.axis_index('right')
    me_l = lax.axis_index('left')
    me = me_r * 4 + me_l
    core = lax.rem(me_l, 2)
    chip = me_l // 2
    mate = chip * 2 + 1 - core
    across = (1 - chip) * 2 + core
    own = pl.ds(pl.multiple_of(me_r * bl, bl), bl)
    half = W // 2
    trips = W // CH
    low = lax.broadcasted_iota(jnp.int32, (8, lt), 0) < 4

    def get_l(n):
        tile = lax.rem(n // trips, 8)
        h, who = tile // 4, lax.rem(tile, 4)
        to = lax.rem(chip + 1 - who // 2, 2) * 2 + lax.rem(core + 1 - lax.rem(who, 2), 2)
        col = pl.ds(pl.multiple_of((2 * to + h) * lt, lt), lt)
        slot = lax.rem(n, 2)
        return pltpu.make_async_copy(l3.at[pl.ds(lax.rem(n, trips) * CH, CH), :, col], lb.at[slot], lsem.at[slot])

    def ag_copy(h, off):
        peer = lax.rem(me_r + off, 4)
        return remote(qg.at[h, :, own, :], qg.at[h, :, own, :], ag_s.at[h, off], ag_r.at[h, me_r], peer, me_l)

    def ag_from(h, off):
        peer = lax.rem(me_r + off, 4)
        there = qg.at[h, :, pl.ds(pl.multiple_of(peer * bl, bl), bl), :]
        return remote(there, there, ag_s.at[h, off], ag_r.at[h, peer], peer, me_l)

    def coef(i, shape):
        one = cf[i, 0:1, 0:1]
        return jnp.broadcast_to(one, shape)

    def update(h, j):
        for off in range(1, 4):
            ag_from(h, off).wait_recv()
            ag_copy(h, off).wait_send()

        for s in range(S):
            vp[h, s] = vg[h, s, own, :]
        chunk = min(256, nb)

        @pl.loop(0, S * (nb // chunk))
        def _(i):
            s = i // (nb // chunk)
            at = pl.ds(pl.multiple_of(lax.rem(i, nb // chunk) * chunk, chunk), chunk)
            new = (qg[h, s, at, :] - coef(0, (chunk, lt)) * vg[h, s, at, :]) * coef(1, (chunk, lt))
            vg[h, s, at, :] = new
            for k, v in enumerate(split3(new)):
                vgs[k, s, at, :] = v

        @pl.when(j < STEPS - 1)
        def _():
            for off in range(1, 4):
                pl.semaphore_signal(credit.at[h], 1, device_id={'right': lax.rem(me_r + off, 4), 'left': me_l},
                                    device_id_type=pl.DeviceIdType.MESH)

    def w_tile(ub, quad, i):
        base = 80 * quad
        pair = base + 64 + 8 * (i // 2)
        parts = [ub[s, base + 16 * i:base + 16 * i + 16, :] for s in range(S)]
        for s in (0, 2):
            one, two = ub[s, pair:pair + 8, :], ub[s + 1, pair:pair + 8, :]
            if i % 2 == 0:
                parts.append(jnp.where(low, one, pltpu.roll(two, 4, 0)))
            else:
                parts.append(jnp.where(low, pltpu.roll(one, 4, 0), two))
        x = jnp.concatenate(parts, axis=0)
        return jnp.concatenate([*split3(x), jnp.zeros((16, lt), BF)], axis=0)

    def w_finish(quad, g, h):
        even, odd = [], []
        for i in range(W // 2):
            v = [ob[b, 8 * i:8 * i + 8, :] for b in range(4)]
            for dst, b0 in ((even, 0), (even, 2)):
                dst.append(jnp.where(low, v[b0], pltpu.roll(v[b0 + 1], 4, 0)))
            for dst, b0 in ((odd, 0), (odd, 2)):
                dst.append(jnp.where(low, pltpu.roll(v[b0], 4, 0), v[b0 + 1]))
        at = pl.ds(pl.multiple_of(g * 64 + 16 * quad, 16), 16)
        col = pl.ds(pl.multiple_of(h * lt, lt), lt)
        for first, lst in ((0, even), (1, odd)):
            for k, v in enumerate(split3(jnp.concatenate(lst, axis=0))):
                for i in range(W // 2):
                    u2[2 * i + first, k, at, col] = v[16 * i:16 * i + 16]

    def group(it, ub_new, ub_old, do_r=True):
        before = lax.rem(it + 2 * groups - 1, 2 * groups)
        gw, hw = lax.rem(before, groups), before // groups
        at = pl.ds(pl.multiple_of(lax.rem(it, groups) * (16 * W), 16 * W), 16 * W)
        for s in range(S):
            if do_r:
                total = None
                for k in range(3):
                    for i in range(3 - k):
                        term = jnp.dot(rts[i, at, :], vgs[k, s], preferred_element_type=F32)
                        total = term if total is None else total + term
                ub_new[s] = total
            for i in range(4):
                y = jnp.dot(wl[...], w_tile(ub_old, s, i), preferred_element_type=F32)
                ob[i] = (y[:4 * W] + y[4 * W:8 * W]) + y[8 * W:]
            w_finish(s, gw, hw)

    def l_trip(n):
        get_l(n).wait()
        get_l(n + 1).start()
        slot, l0 = lax.rem(n, 2), lax.rem(n, trips) * CH
        total = None
        for m in range(CH):
            right = split3(lb[slot, m])
            for k in range(3):
                for i in range(3 - k):
                    term = jnp.dot(u2[l0 + m, i], right[k], preferred_element_type=F32)
                    total = term if total is None else total + term
        acc[...] += total

    def rs_copy(k, h):
        dst = (rb0, xs.at[h], yb)[k]
        i = 1 + h if k == 1 else (0 if k == 0 else 3)
        return remote(sb.at[k], dst, rs_s.at[k], rs_r.at[i], me_r, across if k == 1 else mate)

    def part_of(i):
        return acc[:, i * lw:(i + 1) * lw]

    def send_on(n, j):
        h, who = n // 4, lax.rem(n, 4)

        @pl.when(who == 0)
        def _():
            for i in range(nl):
                sb[0, i] = part_of(i)
            rs_copy(0, h).start()

        @pl.when(who == 1)
        def _():
            rs_copy(0, h).wait_recv()
            for i in range(nl):
                sb[1, i] = part_of(i) + rb0[i]
            rs_copy(1, h).start()

        @pl.when(who == 2)
        def _():
            rs_copy(0, h).wait_send()
            for i in range(nl):
                sb[2, i] = part_of(i)
            rs_copy(2, h).start()

        @pl.when(who == 3)
        def _():
            finish(h, j)

    def finish(h, j):
        rs_copy(2, h).wait_recv()
        rs_copy(1, h).wait_recv()
        for i in range(nl):
            yb[i] = (part_of(i) + yb[i]) + xs[h, i]
        rs_copy(1, h).wait_send()
        rs_copy(2, h).wait_send()
        beta = coef(2, (bl, lt))
        for t in range(S):
            w = jnp.concatenate([yb[i, pl.ds(t, bl, stride=4), :] for i in range(nl)], axis=1)
            al[...] += fold(w * vg[h, t, own, :])
            qg[h, t, own, :] = w - beta * vp[h, t]

        @pl.when(j < STEPS - 1)
        def _():
            pl.semaphore_wait(credit.at[h], 3)
            for off in range(1, 4):
                ag_copy(h, off).start()

    own_psi = pltpu.make_async_copy(psi, qg.at[:, :, own, :], qsem)
    own_psi.start()

    def get_r(i, slot):
        return pltpu.make_async_copy(rtf.at[:, pl.ds(pl.multiple_of(i * 8, 8), 8), :], rcb.at[slot], rcsem.at[slot])

    def r_half(off, peer):
        to = lax.rem(me_r + off, 4)
        part = pl.ds(core * half, half)
        return remote(rbt.at[part, pl.ds(pl.multiple_of(to * bl, bl), bl), :],
                      rtf.at[part, :, pl.ds(pl.multiple_of(peer * bl, bl), bl)], rh_s.at[off], rh_r.at[peer], to, me_l)

    def r_pass(off, which):
        peer = lax.rem(me_r + off, 4)
        part = rtf.at[pl.ds(which * half, half), :, pl.ds(pl.multiple_of(peer * bl, bl), bl)]
        return remote(part, part, rf_s.at[off], rf_r.at[off], me_r, mate)

    def r_own():
        return remote(rbt.at[:, own, :], rtf.at[:, :, own], ro_s.at[0], ro_r.at[0], me_r, mate)

    enter(me)
    for off in range(1, 4):
        r_half(off, me_r).start()
    r_own().start()
    own_psi.wait()
    for h in range(2):
        for off in range(1, 4):
            ag_copy(h, off).start()
    get_l(0).start()

    part = jnp.zeros((8, 128), F32)
    for h in range(2):
        for s in range(S):
            x = qg[h, s, own, :]
            part = part + fold(x * x)
    norm = jnp.sqrt(jnp.broadcast_to(all_sum(part, 0, me, ars, arr, ar_s, ar_r), (8, 128)) / cfg.elems)
    cf[0] = jnp.zeros((8, 128), F32)
    cf[1] = 1.0 / norm
    cf[2] = norm
    vg[...] = jnp.zeros(vg.shape, F32)
    ub1[...] = jnp.zeros(ub1.shape, F32)
    lowb = lax.broadcasted_iota(jnp.int32, (8, nb), 0) < 4

    for off in range(1, 4):
        r_half(off, lax.rem(me_r + off, 4)).wait_recv()
        r_pass(off, core).start()
    r_own().wait_recv()
    for off in range(1, 4):
        r_pass(off, 1 - core).wait_recv()

    @pl.loop(0, bl // 8)
    def _(i):
        slot = 0
        get_r(i, slot).start()
        get_r(i, slot).wait()
        one = jnp.transpose(rcb[slot, 0:8], (1, 0, 2))
        two = jnp.transpose(rcb[slot, 8:16], (1, 0, 2))
        tail = rcb[slot, 16:20]
        tail = jnp.transpose(jnp.concatenate([tail, tail], axis=0), (1, 0, 2))
        for quad in range(2):
            b0 = 4 * quad
            parts = []
            for b in range(b0, b0 + 4):
                parts += [one[b], two[b]]
            parts += [jnp.where(lowb, tail[b0], tail[b0 + 1]), jnp.where(lowb, tail[b0 + 2], tail[b0 + 3])]
            for k, v in enumerate(split3(jnp.concatenate(parts, axis=0))):
                rts[k, pl.ds(pl.multiple_of(i * 160 + 80 * quad, 16), 80), :] = v

    for off in range(1, 4):
        r_half(off, me_r).wait_send()
        r_pass(off, core).wait_send()
    r_own().wait_send()

    @pl.loop(0, STEPS)
    def _(j):
        @pl.loop(0, groups)
        def _(p):
            @pl.when(lax.rem(p, groups // 2) == 0)
            def _():
                update(p // (groups // 2), j)

            group(2 * p, ub0, ub1)
            group(2 * p + 1, ub1, ub0)

        group(2 * groups, ub0, ub1, do_r=False)
        al[...] = jnp.zeros((8, 128), F32)

        acc[...] = jnp.zeros((rows, lt), F32)

        @pl.loop(0, 8 * trips)
        def _(n):
            l_trip(n)

            @pl.when(lax.rem(n, trips) == trips - 1)
            def _():
                send_on(n // trips, j)
                acc[...] = jnp.zeros((rows, lt), F32)

        alpha = jnp.broadcast_to(all_sum(al[...], 0, me, ars, arr, ar_s, ar_r), (8, 128)) / cfg.elems
        cf[0] = alpha
        out_s[j] = alpha
        part = jnp.zeros((8, 128), F32)
        for h in range(2):
            for s in range(S):
                w = qg[h, s, own, :] - coef(0, (bl, lt)) * vg[h, s, own, :]
                part = part + fold(w * w)
        beta = jnp.sqrt(jnp.broadcast_to(all_sum(part, 1, me, ars, arr, ar_s, ar_r), (8, 128)) / cfg.elems)
        cf[1] = 1.0 / beta
        cf[2] = beta
        out_s[STEPS + j] = beta

    get_l(0).wait()
    for h in range(2):
        for s in range(S):
            qg[h, s, own, :] = (qg[h, s, own, :] - coef(0, (bl, lt)) * vg[h, s, own, :]) * coef(1, (bl, lt))
    result = pltpu.make_async_copy(qg.at[:, :, own, :], out_v, qsem)
    result.start()
    result.wait()


def steps(cfg, l3, rbt, psi, wl):
    lt, bl, nb, rows = cfg.lt, cfg.bl, cfg.nb, cfg.rows
    hbm = pl.BlockSpec(memory_space=pl.ANY)
    vm = pl.BlockSpec(memory_space=pltpu.VMEM)
    dma = pltpu.SemaphoreType.DMA
    block = (cfg.nl, rows, lt // cfg.nl)
    scratch = [
        pltpu.VMEM((W, 3, rows, cfg.a), BF),
        pltpu.VMEM((3, W * bl, nb), BF),
        pltpu.VMEM((3, S, nb, lt), BF),
        pltpu.VMEM((2, S, nb, lt), F32),
        pltpu.VMEM((2, S, nb, lt), F32),
        pltpu.VMEM((2, CH, cfg.a, lt), F32),
        pltpu.VMEM((3, *block), F32),
        pltpu.VMEM(block, F32),
        pltpu.VMEM(block, F32),
        pltpu.VMEM((2, *block), F32),
        pltpu.VMEM((S, 16 * W, lt), F32),
        pltpu.VMEM((S, 16 * W, lt), F32),
        pltpu.VMEM((4, 4 * W, lt), F32),
        pltpu.VMEM((2, S, bl, lt), F32),
        pltpu.VMEM((rows, lt), F32),
        pltpu.VMEM((1, W, 8, nb), F32),
        pltpu.VMEM((3, 8, 128), F32),
        pltpu.VMEM((8, 128), F32),
        pltpu.VMEM((2, 8, 128), F32),
        pltpu.VMEM((2, 16, 8, 128), F32),
        dma((2,)), dma((2,)), dma, dma((2, 16)), dma((2, 16)), dma((3,)), dma((4,)), dma((2, 4)), dma((2, 4)),
        dma((4,)), dma((4,)), dma((1,)), dma((1,)), dma((4,)), dma((4,)),
        pltpu.SemaphoreType.REGULAR((2,)),
    ]
    return pl.pallas_call(
        functools.partial(kernel, cfg),
        out_shape=(
            jax.ShapeDtypeStruct((2, S, bl, lt), F32),
            jax.ShapeDtypeStruct((2 * STEPS, 8, 128), F32),
            jax.ShapeDtypeStruct((W, bl, nb), F32),
        ),
        in_specs=[hbm, hbm, hbm, vm],
        out_specs=(hbm, vm, hbm),
        scratch_shapes=scratch,
        compiler_params=pltpu.CompilerParams(collective_id=0, has_side_effects=True, vmem_limit_bytes=VM_LIMIT),
    )(l3, rbt, psi, wl)


def mpo_rows(mpo_two):
    w = mpo_two.reshape(W, W, S, S).transpose(0, 3, 2, 1)
    w = jnp.concatenate([w[..., :16].reshape(W * S, 64), w[..., 16:].reshape(W * S, 16)], axis=1)
    one = lax.reduce_precision(w, 8, 7)
    two = lax.reduce_precision(w - one, 8, 7)
    three = w - one - two
    none = jnp.zeros_like(w)
    left = jnp.concatenate([
        jnp.concatenate([one, one, one], 1),
        jnp.concatenate([two, two, none], 1),
        jnp.concatenate([three, none, none], 1)], 0)
    return jnp.pad(left, ((0, 0), (0, 16))).astype(BF)


def build(mesh, cfg):
    def lanczos(psi_block, left_env, right_env, mpo_two):
        lt, a, bl = cfg.lt, cfg.a, cfg.bl
        l3 = jnp.transpose(left_env, (1, 0, 2))
        rbt = jnp.transpose(right_env, (1, 2, 0))
        psi = psi_block.reshape(2, lt, S, bl).transpose(0, 2, 3, 1)
        wl = mpo_rows(mpo_two)
        vec, scal, _ = steps(cfg, l3, rbt, psi, wl)
        vec = vec.transpose(0, 3, 1, 2).reshape(psi_block.shape)
        return scal[:STEPS, 0, 0], scal[STEPS:, 0, 0], vec

    return jax.shard_map(
        lanczos,
        mesh=mesh,
        in_specs=(P('left', None, None, 'right'), P('left', None, None), P('right', None, None), P()),
        out_specs=(P(), P(), P('left', None, None, 'right')),
        check_vma=False,
    )


def solution(mesh):
    return build(mesh, Cfg())
```

time: 1060 us -> 963 us (0.908)
  Pallas kernels: 1040 us -> 946 us
    pallas_call x2 -> x1, Pallas kernels: 1040 us -> 946 us  [steps(): pl.pallas_call(functools.partial(kernel, cfg), out_shape=(jax.ShapeDtypeS...]
where the time goes in v3:
time: 963 us; the launch traced here: 962 us
  Pallas kernels  946 us (98%)
  local copies, waits for them, and re-layouts  14.9 us (2%)
    pallas_call x1, Pallas kernels, steps(): pl.pallas_call(functools.partial(kernel, cfg), out_shape=(jax.ShapeDtypeS...  946 us

profile of v3, /device:TPU:0, one launch (start us, length us, event | category | flops | bytes accessed | tf_op | source)
XLA Modules:
  0.0 962.2 jit_solution(2909492094842831465)
XLA Ops:
  0.6 0.0 copy-start
  0.6 1.7 copy.12
  2.4 0.1 slice.16
  2.4 0.2 reshape.26
  2.7 0.1 reshape.24
  2.8 0.1 copy.19
  2.8 0.1 copy.14
  2.9 0.1 reduce-precision_convert_fusion.1
  3.0 0.1 fusion.1
  3.2 0.7 pad.7.wl
  3.8 0.0 copy-done
  3.8 1.3 copy.11
  5.2 5.9 copy.9
  11.1 946.4 %shard_map.67 = (f32[2,4,128,256]{3,2,1,0:T(8,128)}, f32[8,8,128]{2,1,0:T(8,128)}, f32[20,128,512]{2,1,0:T(8,128)}) custom-call(f32[20,512,2048]{2,1,0:T(8,128)} %bitcast.l3, f32[20,512,128]{2,1,0:T(8,128)} %bitcast.12, f32[2,4,128,256]{3,2,1,0:T(8,128)} %bitcast.13, bf16[240,256]{1,0:T(8,128)(2,1)} %pad.7.wl), custom_call_target="tpu_custom_call" | custom-call | tf_op jit(solution)/shard_map/pallas_call | solution.py:423
  957.5 1.4 slice_reduce_fusion
  958.9 1.6 copy.15
  960.4 1.8 copy.16
  (2 shorter events, 0.0 us)
Async XLA Ops:
  0.6 3.2 copy-start

commit v4 on v3

--- a/solution.py
+++ b/solution.py
@@ -53,32 +53,37 @@
     pl.semaphore_wait(barrier, 15)
 
 
-def all_sum(part, k, me, out_ref, in_ref, send_sem, recv_sem):
-    out_ref[k] = part
-    in_ref[k, me] = part
-
-    def copy(peer, slot):
-        return remote(out_ref.at[k], in_ref.at[k, slot], send_sem.at[k, peer], recv_sem.at[k, slot],
-                      peer // 4, lax.rem(peer, 4))
+def sum_copy(k, me, peer, slot, out_ref, in_ref, send_sem, recv_sem):
+    return remote(out_ref.at[k], in_ref.at[k, slot], send_sem.at[k, peer], recv_sem.at[k, slot], peer // 4, lax.rem(peer, 4))
+
+
+def sum_start(parts, k, me, *refs):
+    out_ref, in_ref = refs[:2]
+    for i, part in enumerate(parts):
+        out_ref[k, 8 * i:8 * i + 8] = part
+        in_ref[k, me, 8 * i:8 * i + 8] = part
 
     @pl.loop(1, 16)
     def _(off):
-        copy(lax.rem(me + off, 16), me).start()
-
+        sum_copy(k, me, lax.rem(me + off, 16), me, *refs).start()
+
+
+def sum_end(k, me, *refs):
     @pl.loop(1, 16)
     def _(off):
         peer = lax.rem(me + off, 16)
-        copy(peer, peer).wait_recv()
-
-    total = in_ref[k, 0]
+        sum_copy(k, me, peer, peer, *refs).wait_recv()
+
+    total = refs[1][k, 0]
     for i in range(1, 16):
-        total = total + in_ref[k, i]
+        total = total + refs[1][k, i]
 
     @pl.loop(1, 16)
     def _(off):
-        copy(lax.rem(me + off, 16), me).wait_send()
-
-    return jnp.sum(jnp.sum(total, axis=1, keepdims=True), axis=0, keepdims=True)
+        sum_copy(k, me, lax.rem(me + off, 16), me, *refs).wait_send()
+
+    total = jnp.sum(total, axis=1, keepdims=True)
+    return [jnp.broadcast_to(jnp.sum(total[8 * i:8 * i + 8], axis=0, keepdims=True), (8, 128)) for i in range(2)]
 
 
 def fold(x):
@@ -92,11 +97,11 @@
     return jnp.full((8, 128), jnp.sum(x) / 1024.0, F32)
 
 
-CH = 5
+CH = 10
 
 
 def kernel(cfg, l3, rbt, psi, wl, out_v, out_s, rtf,
-           u2, rts, vgs, vg, qg, lb, sb, rb0, yb, xs, ub0, ub1, ob, vp, acc, rcb, cf, al, ars, arr,
+           u2, rts, vgs, vg, qg, lb, sb, rb0, yb, xs, ob, vp, acc, cf, al, ars, arr,
            lsem, rcsem, qsem, ar_s, ar_r, rs_s, rs_r, ag_s, ag_r, rh_s, rh_r, ro_s, ro_r, rf_s, rf_r, credit):
     lt, bl, nb, kb, rows, groups = cfg.lt, cfg.bl, cfg.nb, cfg.kb, cfg.rows, cfg.groups
     nl, lw = cfg.nl, cfg.lt // cfg.nl
@@ -109,6 +114,10 @@
     across = (1 - chip) * 2 + core
     own = pl.ds(pl.multiple_of(me_r * bl, bl), bl)
     half = W // 2
+    ub0 = lb.at[1, 0:S, 0:16 * W]
+    ub1 = lb.at[1, S:2 * S, 0:16 * W]
+    sums = (me, ars, arr, ar_s, ar_r)
+    zero = jnp.zeros((8, 128), F32)
     trips = W // CH
     low = lax.broadcasted_iota(jnp.int32, (8, lt), 0) < 4
 
@@ -167,7 +176,7 @@
                 parts.append(jnp.where(low, one, pltpu.roll(two, 4, 0)))
             else:
                 parts.append(jnp.where(low, pltpu.roll(one, 4, 0), two))
-        x = jnp.concatenate(parts, axis=0)
+        x = jnp.concatenate(parts, axis=0) * coef(3, (4 * W, lt))
         return jnp.concatenate([*split3(x), jnp.zeros((16, lt), BF)], axis=0)
 
     def w_finish(quad, g, h):
@@ -181,11 +190,10 @@
         at = pl.ds(pl.multiple_of(g * 64 + 16 * quad, 16), 16)
         col = pl.ds(pl.multiple_of(h * lt, lt), lt)
         for first, lst in ((0, even), (1, odd)):
-            for k, v in enumerate(split3(jnp.concatenate(lst, axis=0))):
-                for i in range(W // 2):
-                    u2[2 * i + first, k, at, col] = v[16 * i:16 * i + 16]
-
-    def group(it, ub_new, ub_old, do_r=True):
+            for i in range(W // 2):
+                u2[2 * i + first, at, col] = jnp.concatenate(lst[2 * i:2 * i + 2], axis=0)
+
+    def group(it, ub_new, ub_old, do_r=True, do_w=True):
         before = lax.rem(it + 2 * groups - 1, 2 * groups)
         gw, hw = lax.rem(before, groups), before // groups
         at = pl.ds(pl.multiple_of(lax.rem(it, groups) * (16 * W), 16 * W), 16 * W)
@@ -197,6 +205,8 @@
                         term = jnp.dot(rts[i, at, :], vgs[k, s], preferred_element_type=F32)
                         total = term if total is None else total + term
                 ub_new[s] = total
+            if not do_w:
+                continue
             for i in range(4):
                 y = jnp.dot(wl[...], w_tile(ub_old, s, i), preferred_element_type=F32)
                 ob[i] = (y[:4 * W] + y[4 * W:8 * W]) + y[8 * W:]
@@ -208,10 +218,10 @@
         slot, l0 = lax.rem(n, 2), lax.rem(n, trips) * CH
         total = None
         for m in range(CH):
-            right = split3(lb[slot, m])
+            left, right = split3(u2[l0 + m]), split3(lb[slot, m])
             for k in range(3):
                 for i in range(3 - k):
-                    term = jnp.dot(u2[l0 + m, i], right[k], preferred_element_type=F32)
+                    term = jnp.dot(left[i], right[k], preferred_element_type=F32)
                     total = term if total is None else total + term
         acc[...] += total
 
@@ -257,60 +267,74 @@
             yb[i] = (part_of(i) + yb[i]) + xs[h, i]
         rs_copy(1, h).wait_send()
         rs_copy(2, h).wait_send()
-        beta = coef(2, (bl, lt))
         for t in range(S):
             w = jnp.concatenate([yb[i, pl.ds(t, bl, stride=4), :] for i in range(nl)], axis=1)
-            al[...] += fold(w * vg[h, t, own, :])
-            qg[h, t, own, :] = w - beta * vp[h, t]
-
-        @pl.when(j < STEPS - 1)
-        def _():
-            pl.semaphore_wait(credit.at[h], 3)
-            for off in range(1, 4):
-                ag_copy(h, off).start()
+            q = w - coef(2, (bl, lt)) * vp[h, t]
+            al[0:8] += fold(w * vg[h, t, own, :])
+            al[8:16] += fold(q * q)
+            qg[h, t, own, :] = q
+
+        @pl.when((j < STEPS - 1) & (h == 0))
+        def _():
+            ag_start(0)
+
+    def ag_start(h):
+        pl.semaphore_wait(credit.at[h], 3)
+        for off in range(1, 4):
+            ag_copy(h, off).start()
 
     own_psi = pltpu.make_async_copy(psi, qg.at[:, :, own, :], qsem)
     own_psi.start()
 
-    def get_r(i, slot):
-        return pltpu.make_async_copy(rtf.at[:, pl.ds(pl.multiple_of(i * 8, 8), 8), :], rcb.at[slot], rcsem.at[slot])
+    def get_r(i):
+        stage = (ub0, ub1)[i % 2]
+        return pltpu.make_async_copy(rtf.at[i], stage.at[0:2], rcsem.at[i % 2])
+
+    lanes = nb // 2
+    per = lanes // bl
+
+    def columns(peer):
+        return peer // per, pl.ds(pl.multiple_of(lax.rem(peer, per) * bl, bl), bl)
 
     def r_half(off, peer):
         to = lax.rem(me_r + off, 4)
-        part = pl.ds(core * half, half)
-        return remote(rbt.at[part, pl.ds(pl.multiple_of(to * bl, bl), bl), :],
-                      rtf.at[part, :, pl.ds(pl.multiple_of(peer * bl, bl), bl)], rh_s.at[off], rh_r.at[peer], to, me_l)
+        part = pl.ds(pl.multiple_of(core * (8 * W), 8 * W), 8 * W)
+        e, col = columns(peer)
+        return remote(rbt.at[pl.ds(to * groups, groups), part, :], rtf.at[:, e, part, col],
+                      rh_s.at[off], rh_r.at[peer], to, me_l)
 
     def r_pass(off, which):
-        peer = lax.rem(me_r + off, 4)
-        part = rtf.at[pl.ds(which * half, half), :, pl.ds(pl.multiple_of(peer * bl, bl), bl)]
+        e, col = columns(lax.rem(me_r + off, 4))
+        part = rtf.at[:, e, pl.ds(pl.multiple_of(which * (8 * W), 8 * W), 8 * W), col]
         return remote(part, part, rf_s.at[off], rf_r.at[off], me_r, mate)
 
     def r_own():
-        return remote(rbt.at[:, own, :], rtf.at[:, :, own], ro_s.at[0], ro_r.at[0], me_r, mate)
+        e, col = columns(me_r)
+        return remote(rbt.at[pl.ds(me_r * groups, groups)], rtf.at[:, e, :, col], ro_s.at[0], ro_r.at[0], me_r, mate)
 
     enter(me)
+    own_psi.wait()
+    part = zero
+    for h in range(2):
+        for s in range(S):
+            x = qg[h, s, own, :]
+            part = part + fold(x * x)
+    sum_start((part, zero), 2, *sums)
     for off in range(1, 4):
         r_half(off, me_r).start()
     r_own().start()
-    own_psi.wait()
     for h in range(2):
         for off in range(1, 4):
             ag_copy(h, off).start()
     get_l(0).start()
-
-    part = jnp.zeros((8, 128), F32)
-    for h in range(2):
-        for s in range(S):
-            x = qg[h, s, own, :]
-            part = part + fold(x * x)
-    norm = jnp.sqrt(jnp.broadcast_to(all_sum(part, 0, me, ars, arr, ar_s, ar_r), (8, 128)) / cfg.elems)
-    cf[0] = jnp.zeros((8, 128), F32)
+    vg[...] = jnp.zeros(vg.shape, F32)
+    norm = jnp.sqrt(sum_end(2, *sums)[0] / cfg.elems)
+    cf[0] = zero
     cf[1] = 1.0 / norm
-    cf[2] = norm
-    vg[...] = jnp.zeros(vg.shape, F32)
-    ub1[...] = jnp.zeros(ub1.shape, F32)
-    lowb = lax.broadcasted_iota(jnp.int32, (8, nb), 0) < 4
+    cf[2] = zero
+    cf[3] = zero + 1.0
+    cf[4] = norm
+    lowb = lax.broadcasted_iota(jnp.int32, (8, lanes), 0) < 4
 
     for off in range(1, 4):
         r_half(off, lax.rem(me_r + off, 4)).wait_recv()
@@ -318,44 +342,73 @@
     r_own().wait_recv()
     for off in range(1, 4):
         r_pass(off, 1 - core).wait_recv()
-
-    @pl.loop(0, bl // 8)
-    def _(i):
-        slot = 0
-        get_r(i, slot).start()
-        get_r(i, slot).wait()
-        one = jnp.transpose(rcb[slot, 0:8], (1, 0, 2))
-        two = jnp.transpose(rcb[slot, 8:16], (1, 0, 2))
-        tail = rcb[slot, 16:20]
-        tail = jnp.transpose(jnp.concatenate([tail, tail], axis=0), (1, 0, 2))
-        for quad in range(2):
-            b0 = 4 * quad
-            parts = []
-            for b in range(b0, b0 + 4):
-                parts += [one[b], two[b]]
-            parts += [jnp.where(lowb, tail[b0], tail[b0 + 1]), jnp.where(lowb, tail[b0 + 2], tail[b0 + 3])]
-            for k, v in enumerate(split3(jnp.concatenate(parts, axis=0))):
-                rts[k, pl.ds(pl.multiple_of(i * 160 + 80 * quad, 16), 80), :] = v
+    get_r(0).start()
+    for i in range(groups):
+        if i + 1 < groups:
+            get_r(i + 1).start()
+        get_r(i).wait()
+        stage = (ub0, ub1)[i % 2]
+
+        @pl.loop(0, 2)
+        def _(e):
+            raw = stage[e].reshape(W, 16, lanes)
+            for b8 in range(2):
+                cols = raw[:, 8 * b8:8 * b8 + 8]
+                one = jnp.transpose(cols[0:8], (1, 0, 2))
+                two = jnp.transpose(cols[8:16], (1, 0, 2))
+                tail = jnp.transpose(jnp.concatenate([cols[16:20], cols[16:20]], axis=0), (1, 0, 2))
+                for quad in range(2):
+                    b0 = 4 * quad
+                    parts = []
+                    for b in range(b0, b0 + 4):
+                        parts += [one[b], two[b]]
+                    parts += [jnp.where(lowb, tail[b0], tail[b0 + 1]), jnp.where(lowb, tail[b0 + 2], tail[b0 + 3])]
+                    row = i * 320 + 160 * b8 + 80 * quad
+                    for k, v in enumerate(split3(jnp.concatenate(parts, axis=0))):
+                        rts[k, row:row + 80, pl.ds(pl.multiple_of(e * lanes, lanes), lanes)] = v
 
     for off in range(1, 4):
         r_half(off, me_r).wait_send()
         r_pass(off, core).wait_send()
     r_own().wait_send()
 
+    def norm_start():
+        part = zero
+        for h in range(2):
+            for s in range(S):
+                w = (qg[h, s, own, :] - coef(0, (bl, lt)) * vg[h, s, own, :]) * coef(1, (bl, lt))
+                part = part + fold(w * w)
+        sum_start((part, zero), 1, *sums)
+
+    def norm_end(j):
+        gamma = jnp.sqrt(sum_end(1, *sums)[0] / cfg.elems)
+        beta = gamma * cf[4]
+        out_s[STEPS + j] = beta
+        cf[2] = beta * cf[3]
+        cf[3] = 1.0 / gamma
+
     @pl.loop(0, STEPS)
     def _(j):
-        @pl.loop(0, groups)
+        update(0, j)
+        group(0, ub0, ub1, do_w=False)
+
+        @pl.when(j > 0)
+        def _():
+            norm_end(j - 1)
+
+        group(1, ub1, ub0)
+
+        @pl.loop(1, groups)
         def _(p):
-            @pl.when(lax.rem(p, groups // 2) == 0)
+            @pl.when(p == groups // 2)
             def _():
-                update(p // (groups // 2), j)
+                update(1, j)
 
             group(2 * p, ub0, ub1)
             group(2 * p + 1, ub1, ub0)
 
         group(2 * groups, ub0, ub1, do_r=False)
-        al[...] = jnp.zeros((8, 128), F32)
-
+        al[...] = jnp.zeros((16, 128), F32)
         acc[...] = jnp.zeros((rows, lt), F32)
 
         @pl.loop(0, 8 * trips)
@@ -367,23 +420,27 @@
                 send_on(n // trips, j)
                 acc[...] = jnp.zeros((rows, lt), F32)
 
-        alpha = jnp.broadcast_to(all_sum(al[...], 0, me, ars, arr, ar_s, ar_r), (8, 128)) / cfg.elems
-        cf[0] = alpha
+        sum_start((al[0:8], al[8:16]), 0, *sums)
+        dot, square = sum_end(0, *sums)
+        alpha = cf[3] * (dot / cfg.elems)
+        size = jnp.sqrt(square / cfg.elems)
+        size = jnp.where(size > 0.0, size, 1.0)
         out_s[j] = alpha
-        part = jnp.zeros((8, 128), F32)
-        for h in range(2):
-            for s in range(S):
-                w = qg[h, s, own, :] - coef(0, (bl, lt)) * vg[h, s, own, :]
-                part = part + fold(w * w)
-        beta = jnp.sqrt(jnp.broadcast_to(all_sum(part, 1, me, ars, arr, ar_s, ar_r), (8, 128)) / cfg.elems)
-        cf[1] = 1.0 / beta
-        cf[2] = beta
-        out_s[STEPS + j] = beta
-
+        cf[0] = alpha * cf[3]
+        cf[1] = 1.0 / size
+        cf[4] = size
+        norm_start()
+
+        @pl.when(j < STEPS - 1)
+        def _():
+            ag_start(1)
+
+    norm_end(STEPS - 1)
     get_l(0).wait()
     for h in range(2):
         for s in range(S):
-            qg[h, s, own, :] = (qg[h, s, own, :] - coef(0, (bl, lt)) * vg[h, s, own, :]) * coef(1, (bl, lt))
+            v = (qg[h, s, own, :] - coef(0, (bl, lt)) * vg[h, s, own, :]) * coef(1, (bl, lt))
+            qg[h, s, own, :] = v * coef(3, (bl, lt))
     result = pltpu.make_async_copy(qg.at[:, :, own, :], out_v, qsem)
     result.start()
     result.wait()
@@ -396,7 +453,7 @@
     dma = pltpu.SemaphoreType.DMA
     block = (cfg.nl, rows, lt // cfg.nl)
     scratch = [
-        pltpu.VMEM((W, 3, rows, cfg.a), BF),
+        pltpu.VMEM((W, rows, cfg.a), F32),
         pltpu.VMEM((3, W * bl, nb), BF),
         pltpu.VMEM((3, S, nb, lt), BF),
         pltpu.VMEM((2, S, nb, lt), F32),
@@ -406,17 +463,14 @@
         pltpu.VMEM(block, F32),
         pltpu.VMEM(block, F32),
         pltpu.VMEM((2, *block), F32),
-        pltpu.VMEM((S, 16 * W, lt), F32),
-        pltpu.VMEM((S, 16 * W, lt), F32),
         pltpu.VMEM((4, 4 * W, lt), F32),
         pltpu.VMEM((2, S, bl, lt), F32),
         pltpu.VMEM((rows, lt), F32),
-        pltpu.VMEM((1, W, 8, nb), F32),
-        pltpu.VMEM((3, 8, 128), F32),
-        pltpu.VMEM((8, 128), F32),
-        pltpu.VMEM((2, 8, 128), F32),
-        pltpu.VMEM((2, 16, 8, 128), F32),
-        dma((2,)), dma((2,)), dma, dma((2, 16)), dma((2, 16)), dma((3,)), dma((4,)), dma((2, 4)), dma((2, 4)),
+        pltpu.VMEM((5, 8, 128), F32),
+        pltpu.VMEM((16, 128), F32),
+        pltpu.VMEM((3, 16, 128), F32),
+        pltpu.VMEM((3, 16, 16, 128), F32),
+        dma((2,)), dma((2,)), dma, dma((3, 16)), dma((3, 16)), dma((3,)), dma((4,)), dma((2, 4)), dma((2, 4)),
         dma((4,)), dma((4,)), dma((1,)), dma((1,)), dma((4,)), dma((4,)),
         pltpu.SemaphoreType.REGULAR((2,)),
     ]
@@ -425,7 +479,7 @@
         out_shape=(
             jax.ShapeDtypeStruct((2, S, bl, lt), F32),
             jax.ShapeDtypeStruct((2 * STEPS, 8, 128), F32),
-            jax.ShapeDtypeStruct((W, bl, nb), F32),
+            jax.ShapeDtypeStruct((cfg.groups, 2, 16 * W, nb // 2), F32),
         ),
         in_specs=[hbm, hbm, hbm, vm],
         out_specs=(hbm, vm, hbm),
@@ -452,7 +506,7 @@
     def lanczos(psi_block, left_env, right_env, mpo_two):
         lt, a, bl = cfg.lt, cfg.a, cfg.bl
         l3 = jnp.transpose(left_env, (1, 0, 2))
-        rbt = jnp.transpose(right_env, (1, 2, 0))
+        rbt = right_env.reshape(bl, W, 4 * cfg.groups, 16).transpose(2, 1, 3, 0).reshape(4 * cfg.groups, 16 * W, bl)
         psi = psi_block.reshape(2, lt, S, bl).transpose(0, 2, 3, 1)
         wl = mpo_rows(mpo_two)
         vec, scal, _ = steps(cfg, l3, rbt, psi, wl)

time: 963 us -> 848 us (0.88)
  Pallas kernels: 946 us -> 826 us
    pallas_call x1, Pallas kernels: 946 us -> 826 us  [steps(): pl.pallas_call(functools.partial(kernel, cfg), out_shape=(jax.ShapeDtypeS...]
where the time goes in v4:
time: 848 us; the launch traced here: 847 us
  Pallas kernels  826 us (97%)
  local copies, waits for them, and re-layouts  20.4 us (2%)
    pallas_call x1, Pallas kernels, steps(): pl.pallas_call(functools.partial(kernel, cfg), out_shape=(jax.ShapeDtypeS...  826 us

profile of v4, /device:TPU:0, one launch (start us, length us, event | category | flops | bytes accessed | tf_op | source)
XLA Modules:
  0.0 847.4 jit_solution(10165782550369159128)
XLA Ops:
  0.6 0.0 copy-start
  0.6 1.7 copy.13
  2.4 0.1 slice.16
  2.4 0.2 reshape.34
  2.7 0.1 reshape.32
  2.8 0.1 copy.20
  2.8 0.1 copy.15
  2.9 0.1 reduce-precision_convert_fusion.1
  3.0 0.1 fusion.1
  3.2 0.7 pad.7.wl
  3.8 0.0 copy-done
  3.8 1.3 copy.12
  5.2 6.0 copy.9
  11.1 5.5 copy.10
  16.6 826.0 %shard_map.67 = (f32[2,4,128,256]{3,2,1,0:T(8,128)}, f32[8,8,128]{2,1,0:T(8,128)}, f32[8,2,320,256]{3,2,1,0:T(8,128)}) custom-call(f32[20,512,2048]{2,1,0:T(8,128)} %bitcast.l3, f32[32,320,128]{2,1,0:T(8,128)} %bitcast.16, f32[2,4,128,256]{3,2,1,0:T(8,128)} %bitcast.17, bf16[240,256]{1,0:T(8,128)(2,1)} %pad.7.wl), custom_call_target="tpu_custom_call" | custom-call | tf_op jit(solution)/shard_map/pallas_call | solution.py:477
  842.7 1.4 slice_reduce_fusion
  844.0 1.6 copy.16
  845.6 1.8 copy.17
  (2 shorter events, 0.0 us)
Async XLA Ops:
  0.6 3.2 copy-start

commit v5 on v4

--- a/solution.py
+++ b/solution.py
@@ -50,8 +50,6 @@
         pl.semaphore_signal(barrier, 1, device_id={'right': peer // 4, 'left': lax.rem(peer, 4)},
                             device_id_type=pl.DeviceIdType.MESH)
 
-    pl.semaphore_wait(barrier, 15)
-
 
 def sum_copy(k, me, peer, slot, out_ref, in_ref, send_sem, recv_sem):
     return remote(out_ref.at[k], in_ref.at[k, slot], send_sem.at[k, peer], recv_sem.at[k, slot], peer // 4, lax.rem(peer, 4))
@@ -78,12 +76,14 @@
     for i in range(1, 16):
         total = total + refs[1][k, i]
 
+    total = jnp.sum(total, axis=1, keepdims=True)
+    return [jnp.broadcast_to(jnp.sum(total[8 * i:8 * i + 8], axis=0, keepdims=True), (8, 128)) for i in range(2)]
+
+
+def sum_sent(k, me, *refs):
     @pl.loop(1, 16)
     def _(off):
         sum_copy(k, me, lax.rem(me + off, 16), me, *refs).wait_send()
-
-    total = jnp.sum(total, axis=1, keepdims=True)
-    return [jnp.broadcast_to(jnp.sum(total[8 * i:8 * i + 8], axis=0, keepdims=True), (8, 128)) for i in range(2)]
 
 
 def fold(x):
@@ -100,9 +100,9 @@
 CH = 10
 
 
-def kernel(cfg, l3, rbt, psi, wl, out_v, out_s, rtf,
+def kernel(cfg, l3, rb3, psi, wl, out_v, out_s,
            u2, rts, vgs, vg, qg, lb, sb, rb0, yb, xs, ob, vp, acc, cf, al, ars, arr,
-           lsem, rcsem, qsem, ar_s, ar_r, rs_s, rs_r, ag_s, ag_r, rh_s, rh_r, ro_s, ro_r, rf_s, rf_r, credit):
+           lsem, psem, qsem, ar_s, ar_r, rs_s, rs_r, ag_s, ag_r, rh_s, rh_r, rx_s, rx_r, rm_s, rm_r, rn_s, rn_r, credit):
     lt, bl, nb, kb, rows, groups = cfg.lt, cfg.bl, cfg.nb, cfg.kb, cfg.rows, cfg.groups
     nl, lw = cfg.nl, cfg.lt // cfg.nl
     me_r = lax.axis_index('right')
@@ -113,7 +113,6 @@
     mate = chip * 2 + 1 - core
     across = (1 - chip) * 2 + core
     own = pl.ds(pl.multiple_of(me_r * bl, bl), bl)
-    half = W // 2
     ub0 = lb.at[1, 0:S, 0:16 * W]
     ub1 = lb.at[1, S:2 * S, 0:16 * W]
     sums = (me, ars, arr, ar_s, ar_r)
@@ -283,50 +282,62 @@
         for off in range(1, 4):
             ag_copy(h, off).start()
 
-    own_psi = pltpu.make_async_copy(psi, qg.at[:, :, own, :], qsem)
-    own_psi.start()
-
-    def get_r(i):
-        stage = (ub0, ub1)[i % 2]
-        return pltpu.make_async_copy(rtf.at[i], stage.at[0:2], rcsem.at[i % 2])
-
-    lanes = nb // 2
-    per = lanes // bl
-
-    def columns(peer):
-        return peer // per, pl.ds(pl.multiple_of(lax.rem(peer, per) * bl, bl), bl)
-
-    def r_half(off, peer):
+    def get_psi(i):
+        return pltpu.make_async_copy(psi.at[i], sb.at[i // 2, i % 2], psem.at[i])
+
+    load_r = pltpu.make_async_copy(rb3, u2.at[:, 0:bl, :], qsem)
+    load_r.start()
+    for i in range(4):
+        get_psi(i).start()
+    enter(me)
+    part = zero
+    for i in range(4):
+        get_psi(i).wait()
+        for s in range(S):
+            x = sb[i // 2, i % 2, pl.ds(s, bl, stride=S), :]
+            part = part + fold(x * x)
+            qg[i // 2, s, own, (i % 2) * lw:(i % 2 + 1) * lw] = x.T
+    load_r.wait()
+    block = 16 * W
+
+    @pl.loop(0, W)
+    def _(r):
+        at = pl.ds(pl.multiple_of(bl + r * 16, 16), 16)
+        turned = [u2[r, 0:bl, p * bl:(p + 1) * bl].T for p in range(4)]
+        for p, x in enumerate(turned):
+            for g in range(groups):
+                u2[g, at, p * bl:(p + 1) * bl] = x[16 * g:16 * g + 16]
+
+    def to_send(peer, q):
+        return u2.at[0:groups, pl.ds(pl.multiple_of(bl + q * (block // 4), 8), block // 4),
+                     pl.ds(pl.multiple_of(peer * bl, bl), bl)]
+
+    def landed(peer, q):
+        return u2.at[groups:2 * groups, pl.ds(pl.multiple_of(bl + q * (block // 4), 8), block // 4),
+                     pl.ds(pl.multiple_of(peer * bl, bl), bl)]
+
+    def r_quarter(off, peer):
         to = lax.rem(me_r + off, 4)
-        part = pl.ds(pl.multiple_of(core * (8 * W), 8 * W), 8 * W)
-        e, col = columns(peer)
-        return remote(rbt.at[pl.ds(to * groups, groups), part, :], rtf.at[:, e, part, col],
-                      rh_s.at[off], rh_r.at[peer], to, me_l)
-
-    def r_pass(off, which):
-        e, col = columns(lax.rem(me_r + off, 4))
-        part = rtf.at[:, e, pl.ds(pl.multiple_of(which * (8 * W), 8 * W), 8 * W), col]
-        return remote(part, part, rf_s.at[off], rf_r.at[off], me_r, mate)
-
-    def r_own():
-        e, col = columns(me_r)
-        return remote(rbt.at[pl.ds(me_r * groups, groups)], rtf.at[:, e, :, col], ro_s.at[0], ro_r.at[0], me_r, mate)
-
-    enter(me)
-    own_psi.wait()
-    part = zero
-    for h in range(2):
-        for s in range(S):
-            x = qg[h, s, own, :]
-            part = part + fold(x * x)
+        return remote(to_send(to, me_l), landed(peer, me_l), rh_s.at[off], rh_r.at[peer], to, me_l)
+
+    def pass_on(off, q, where, send_sem, recv_sem):
+        part = landed(lax.rem(me_r + off, 4), q)
+        return remote(part, part, send_sem.at[off], recv_sem.at[off], me_r, where)
+
+    pl.semaphore_wait(pltpu.get_barrier_semaphore(), 15)
     sum_start((part, zero), 2, *sums)
     for off in range(1, 4):
-        r_half(off, me_r).start()
-    r_own().start()
+        r_quarter(off, me_r).start()
     for h in range(2):
         for off in range(1, 4):
             ag_copy(h, off).start()
     get_l(0).start()
+
+    @pl.loop(0, groups)
+    def _(g):
+        col = pl.ds(pl.multiple_of(me_r * bl, bl), bl)
+        u2[groups + g, bl:bl + block, col] = u2[g, bl:bl + block, col]
+
     vg[...] = jnp.zeros(vg.shape, F32)
     norm = jnp.sqrt(sum_end(2, *sums)[0] / cfg.elems)
     cf[0] = zero
@@ -334,24 +345,25 @@
     cf[2] = zero
     cf[3] = zero + 1.0
     cf[4] = norm
+    sum_sent(2, *sums)
+    diag = (1 - chip) * 2 + 1 - core
+    for off in range(1, 4):
+        r_quarter(off, lax.rem(me_r + off, 4)).wait_recv()
+        pass_on(off, me_l, across, rx_s, rx_r).start()
+        pass_on(off, me_l, mate, rm_s, rm_r).start()
+    for off in range(1, 4):
+        pass_on(off, across, across, rx_s, rx_r).wait_recv()
+        pass_on(off, across, mate, rn_s, rn_r).start()
+    for off in range(1, 4):
+        pass_on(off, mate, mate, rm_s, rm_r).wait_recv()
+        pass_on(off, diag, mate, rn_s, rn_r).wait_recv()
+    lanes = nb // 2
     lowb = lax.broadcasted_iota(jnp.int32, (8, lanes), 0) < 4
 
-    for off in range(1, 4):
-        r_half(off, lax.rem(me_r + off, 4)).wait_recv()
-        r_pass(off, core).start()
-    r_own().wait_recv()
-    for off in range(1, 4):
-        r_pass(off, 1 - core).wait_recv()
-    get_r(0).start()
-    for i in range(groups):
-        if i + 1 < groups:
-            get_r(i + 1).start()
-        get_r(i).wait()
-        stage = (ub0, ub1)[i % 2]
-
-        @pl.loop(0, 2)
-        def _(e):
-            raw = stage[e].reshape(W, 16, lanes)
+    @pl.loop(0, groups)
+    def _(g):
+        for e in range(2):
+            raw = u2[groups + g, bl:bl + block, e * lanes:(e + 1) * lanes].reshape(W, 16, lanes)
             for b8 in range(2):
                 cols = raw[:, 8 * b8:8 * b8 + 8]
                 one = jnp.transpose(cols[0:8], (1, 0, 2))
@@ -363,14 +375,15 @@
                     for b in range(b0, b0 + 4):
                         parts += [one[b], two[b]]
                     parts += [jnp.where(lowb, tail[b0], tail[b0 + 1]), jnp.where(lowb, tail[b0 + 2], tail[b0 + 3])]
-                    row = i * 320 + 160 * b8 + 80 * quad
+                    at = pl.ds(pl.multiple_of(g * block + 160 * b8 + 80 * quad, 16), 80)
                     for k, v in enumerate(split3(jnp.concatenate(parts, axis=0))):
-                        rts[k, row:row + 80, pl.ds(pl.multiple_of(e * lanes, lanes), lanes)] = v
+                        rts[k, at, e * lanes:(e + 1) * lanes] = v
 
     for off in range(1, 4):
-        r_half(off, me_r).wait_send()
-        r_pass(off, core).wait_send()
-    r_own().wait_send()
+        r_quarter(off, me_r).wait_send()
+        pass_on(off, me_l, across, rx_s, rx_r).wait_send()
+        pass_on(off, me_l, mate, rm_s, rm_r).wait_send()
+        pass_on(off, across, mate, rn_s, rn_r).wait_send()
 
     def norm_start():
         part = zero
@@ -386,6 +399,7 @@
         out_s[STEPS + j] = beta
         cf[2] = beta * cf[3]
         cf[3] = 1.0 / gamma
+        sum_sent(1, *sums)
 
     @pl.loop(0, STEPS)
     def _(j):
@@ -435,6 +449,8 @@
         def _():
             ag_start(1)
 
+        sum_sent(0, *sums)
+
     norm_end(STEPS - 1)
     get_l(0).wait()
     for h in range(2):
@@ -446,7 +462,7 @@
     result.wait()
 
 
-def steps(cfg, l3, rbt, psi, wl):
+def steps(cfg, l3, rb3, psi, wl):
     lt, bl, nb, rows = cfg.lt, cfg.bl, cfg.nb, cfg.rows
     hbm = pl.BlockSpec(memory_space=pl.ANY)
     vm = pl.BlockSpec(memory_space=pltpu.VMEM)
@@ -470,8 +486,8 @@
         pltpu.VMEM((16, 128), F32),
         pltpu.VMEM((3, 16, 128), F32),
         pltpu.VMEM((3, 16, 16, 128), F32),
-        dma((2,)), dma((2,)), dma, dma((3, 16)), dma((3, 16)), dma((3,)), dma((4,)), dma((2, 4)), dma((2, 4)),
-        dma((4,)), dma((4,)), dma((1,)), dma((1,)), dma((4,)), dma((4,)),
+        dma((2,)), dma((4,)), dma, dma((3, 16)), dma((3, 16)), dma((3,)), dma((4,)), dma((2, 4)), dma((2, 4)),
+        dma((4,)), dma((4,)), dma((4,)), dma((4,)), dma((4,)), dma((4,)), dma((4,)), dma((4,)),
         pltpu.SemaphoreType.REGULAR((2,)),
     ]
     return pl.pallas_call(
@@ -479,13 +495,12 @@
         out_shape=(
             jax.ShapeDtypeStruct((2, S, bl, lt), F32),
             jax.ShapeDtypeStruct((2 * STEPS, 8, 128), F32),
-            jax.ShapeDtypeStruct((cfg.groups, 2, 16 * W, nb // 2), F32),
         ),
         in_specs=[hbm, hbm, hbm, vm],
-        out_specs=(hbm, vm, hbm),
+        out_specs=(hbm, vm),
         scratch_shapes=scratch,
         compiler_params=pltpu.CompilerParams(collective_id=0, has_side_effects=True, vmem_limit_bytes=VM_LIMIT),
-    )(l3, rbt, psi, wl)
+    )(l3, rb3, psi, wl)
 
 
 def mpo_rows(mpo_two):
@@ -506,10 +521,10 @@
     def lanczos(psi_block, left_env, right_env, mpo_two):
         lt, a, bl = cfg.lt, cfg.a, cfg.bl
         l3 = jnp.transpose(left_env, (1, 0, 2))
-        rbt = right_env.reshape(bl, W, 4 * cfg.groups, 16).transpose(2, 1, 3, 0).reshape(4 * cfg.groups, 16 * W, bl)
-        psi = psi_block.reshape(2, lt, S, bl).transpose(0, 2, 3, 1)
+        rb3 = jnp.transpose(right_env, (1, 0, 2))
+        psi = psi_block.reshape(4, a, bl)
         wl = mpo_rows(mpo_two)
-        vec, scal, _ = steps(cfg, l3, rbt, psi, wl)
+        vec, scal = steps(cfg, l3, rb3, psi, wl)
         vec = vec.transpose(0, 3, 1, 2).reshape(psi_block.shape)
         return scal[:STEPS, 0, 0], scal[STEPS:, 0, 0], vec
 

time: 848 us -> 822 us (0.969)
  Pallas kernels: 826 us -> 813 us
  local copies, waits for them, and re-layouts: 20.4 us -> 7.55 us
    pallas_call x1, Pallas kernels: 826 us -> 813 us  [steps(): pl.pallas_call(functools.partial(kernel, cfg), out_shape=(jax.ShapeDtypeS...]
where the time goes in v5:
time: 822 us; the launch traced here: 821 us
  Pallas kernels  813 us (99%)
    pallas_call x1, Pallas kernels, steps(): pl.pallas_call(functools.partial(kernel, cfg), out_shape=(jax.ShapeDtypeS...  813 us

profile of v5, /device:TPU:0, one launch (start us, length us, event | category | flops | bytes accessed | tf_op | source)
XLA Modules:
  0.0 821.4 jit_solution(6663467117264963807)
XLA Ops:
  0.6 1.6 copy.8
  2.3 0.1 slice.16
  2.3 0.2 reshape.26
  2.6 0.1 reshape.24
  2.7 0.1 copy.13
  2.8 0.1 copy.10
  2.8 0.1 reduce-precision_convert_fusion.1
  3.0 0.1 fusion.1
  3.1 0.7 pad.7.wl
  3.7 812.9 %shard_map.67 = (f32[2,4,128,256]{3,2,1,0:T(8,128)}, f32[8,8,128]{2,1,0:T(8,128)}) custom-call(f32[20,512,2048]{2,1,0:T(8,128)} %bitcast.l3, f32[20,128,512]{2,1,0:T(8,128)} %bitcast.11, f32[4,512,128]{2,1,0:T(8,128)} %bitcast.15, bf16[240,256]{1,0:T(8,128)(2,1)} %pad.7.wl), custom_call_target="tpu_custom_call" | custom-call | tf_op jit(solution)/shard_map/pallas_call | solution.py:493
  816.7 1.4 slice_reduce_fusion
  818.0 1.6 copy.11
  819.6 1.8 copy.12
  (2 shorter events, 0.0 us)

commit v6 on v5

--- a/solution.py
+++ b/solution.py
@@ -112,6 +112,8 @@
     chip = me_l // 2
     mate = chip * 2 + 1 - core
     across = (1 - chip) * 2 + core
+    diag = (1 - chip) * 2 + 1 - core
+    peers = (me_r, me_r + 1 - 2 * lax.rem(me_r, 2), lax.rem(me_r + 2, 4), 3 - me_r)
     own = pl.ds(pl.multiple_of(me_r * bl, bl), bl)
     ub0 = lb.at[1, 0:S, 0:16 * W]
     ub1 = lb.at[1, S:2 * S, 0:16 * W]
@@ -128,14 +130,12 @@
         slot = lax.rem(n, 2)
         return pltpu.make_async_copy(l3.at[pl.ds(lax.rem(n, trips) * CH, CH), :, col], lb.at[slot], lsem.at[slot])
 
-    def ag_copy(h, off):
-        peer = lax.rem(me_r + off, 4)
-        return remote(qg.at[h, :, own, :], qg.at[h, :, own, :], ag_s.at[h, off], ag_r.at[h, me_r], peer, me_l)
-
-    def ag_from(h, off):
-        peer = lax.rem(me_r + off, 4)
-        there = qg.at[h, :, pl.ds(pl.multiple_of(peer * bl, bl), bl), :]
-        return remote(there, there, ag_s.at[h, off], ag_r.at[h, peer], peer, me_l)
+    def ag_copy(h, k):
+        return remote(qg.at[h, :, own, :], qg.at[h, :, own, :], ag_s.at[h, k], ag_r.at[h, k], peers[k], me_l)
+
+    def ag_from(h, k):
+        there = qg.at[h, :, pl.ds(pl.multiple_of(peers[k] * bl, bl), bl), :]
+        return remote(there, there, ag_s.at[h, k], ag_r.at[h, k], peers[k], me_l)
 
     def coef(i, shape):
         one = cf[i, 0:1, 0:1]
@@ -148,7 +148,7 @@
 
         for s in range(S):
             vp[h, s] = vg[h, s, own, :]
-        chunk = min(256, nb)
+        chunk = min(128, nb)
 
         @pl.loop(0, S * (nb // chunk))
         def _(i):
@@ -162,7 +162,7 @@
         @pl.when(j < STEPS - 1)
         def _():
             for off in range(1, 4):
-                pl.semaphore_signal(credit.at[h], 1, device_id={'right': lax.rem(me_r + off, 4), 'left': me_l},
+                pl.semaphore_signal(credit.at[h], 1, device_id={'right': peers[off], 'left': me_l},
                                     device_id_type=pl.DeviceIdType.MESH)
 
     def w_tile(ub, quad, i):
@@ -316,21 +316,17 @@
         return u2.at[groups:2 * groups, pl.ds(pl.multiple_of(bl + q * (block // 4), 8), block // 4),
                      pl.ds(pl.multiple_of(peer * bl, bl), bl)]
 
-    def r_quarter(off, peer):
-        to = lax.rem(me_r + off, 4)
-        return remote(to_send(to, me_l), landed(peer, me_l), rh_s.at[off], rh_r.at[peer], to, me_l)
-
-    def pass_on(off, q, where, send_sem, recv_sem):
-        part = landed(lax.rem(me_r + off, 4), q)
-        return remote(part, part, send_sem.at[off], recv_sem.at[off], me_r, where)
+    def r_quarter(k, peer):
+        return remote(to_send(peers[k], me_l), landed(peer, me_l), rh_s.at[k], rh_r.at[k], peers[k], me_l)
+
+    def pass_on(k, q, where, send_sem, recv_sem):
+        part = landed(peers[k], q)
+        return remote(part, part, send_sem.at[k], recv_sem.at[k], me_r, where)
 
     pl.semaphore_wait(pltpu.get_barrier_semaphore(), 15)
     sum_start((part, zero), 2, *sums)
     for off in range(1, 4):
         r_quarter(off, me_r).start()
-    for h in range(2):
-        for off in range(1, 4):
-            ag_copy(h, off).start()
     get_l(0).start()
 
     @pl.loop(0, groups)
@@ -346,11 +342,15 @@
     cf[3] = zero + 1.0
     cf[4] = norm
     sum_sent(2, *sums)
-    diag = (1 - chip) * 2 + 1 - core
     for off in range(1, 4):
-        r_quarter(off, lax.rem(me_r + off, 4)).wait_recv()
+        r_quarter(off, peers[off]).wait_recv()
         pass_on(off, me_l, across, rx_s, rx_r).start()
         pass_on(off, me_l, mate, rm_s, rm_r).start()
+    for off in range(1, 4):
+        r_quarter(off, me_r).wait_send()
+    for h in range(2):
+        for off in range(1, 4):
+            ag_copy(h, off).start()
     for off in range(1, 4):
         pass_on(off, across, across, rx_s, rx_r).wait_recv()
         pass_on(off, across, mate, rn_s, rn_r).start()
@@ -380,7 +380,6 @@
                         rts[k, at, e * lanes:(e + 1) * lanes] = v
 
     for off in range(1, 4):
-        r_quarter(off, me_r).wait_send()
         pass_on(off, me_l, across, rx_s, rx_r).wait_send()
         pass_on(off, me_l, mate, rm_s, rm_r).wait_send()
         pass_on(off, across, mate, rn_s, rn_r).wait_send()

time: 822 us -> 824 us (level)
  no operation moved by 1% of the time
where the time goes in v6:
time: 824 us
  Pallas kernels  815 us (99%)
    pallas_call x1, Pallas kernels, steps(): pl.pallas_call(functools.partial(kernel, cfg), out_shape=(jax.ShapeDtypeS...  815 us

profile of v6, /device:TPU:0, one launch (start us, length us, event | category | flops | bytes accessed | tf_op | source)
XLA Modules:
  0.0 823.7 jit_solution(3321478061706483804)
XLA Ops:
  0.6 1.6 copy.8
  2.3 0.1 slice.16
  2.3 0.2 reshape.26
  2.6 0.1 reshape.24
  2.7 0.1 copy.13
  2.8 0.1 copy.10
  2.8 0.1 reduce-precision_convert_fusion.1
  3.0 0.1 fusion.1
  3.1 0.7 pad.7.wl
  3.7 815.3 %shard_map.67 = (f32[2,4,128,256]{3,2,1,0:T(8,128)}, f32[8,8,128]{2,1,0:T(8,128)}) custom-call(f32[20,512,2048]{2,1,0:T(8,128)} %bitcast.l3, f32[20,128,512]{2,1,0:T(8,128)} %bitcast.11, f32[4,512,128]{2,1,0:T(8,128)} %bitcast.15, bf16[240,256]{1,0:T(8,128)(2,1)} %pad.7.wl), custom_call_target="tpu_custom_call" | custom-call | tf_op jit(solution)/shard_map/pallas_call | solution.py:492
  819.0 1.4 slice_reduce_fusion
  820.4 1.6 copy.11
  822.0 1.8 copy.12
  (2 shorter events, 0.0 us)

commit v7 on v6

--- a/solution.py
+++ b/solution.py
@@ -148,7 +148,7 @@
 
         for s in range(S):
             vp[h, s] = vg[h, s, own, :]
-        chunk = min(128, nb)
+        chunk = min(256, nb)
 
         @pl.loop(0, S * (nb // chunk))
         def _(i):
@@ -346,11 +346,9 @@
         r_quarter(off, peers[off]).wait_recv()
         pass_on(off, me_l, across, rx_s, rx_r).start()
         pass_on(off, me_l, mate, rm_s, rm_r).start()
-    for off in range(1, 4):
-        r_quarter(off, me_r).wait_send()
-    for h in range(2):
-        for off in range(1, 4):
-            ag_copy(h, off).start()
+        if off > 1:
+            for k in range(1, 4):
+                ag_copy(off - 2, k).start()
     for off in range(1, 4):
         pass_on(off, across, across, rx_s, rx_r).wait_recv()
         pass_on(off, across, mate, rn_s, rn_r).start()
@@ -380,6 +378,7 @@
                         rts[k, at, e * lanes:(e + 1) * lanes] = v
 
     for off in range(1, 4):
+        r_quarter(off, me_r).wait_send()
         pass_on(off, me_l, across, rx_s, rx_r).wait_send()
         pass_on(off, me_l, mate, rm_s, rm_r).wait_send()
         pass_on(off, across, mate, rn_s, rn_r).wait_send()

time: 824 us -> 823 us (level)
  no operation moved by 1% of the time
where the time goes in v7:
time: 823 us; the launch traced here: 822 us
  Pallas kernels  814 us (99%)
    pallas_call x1, Pallas kernels, steps(): pl.pallas_call(functools.partial(kernel, cfg), out_shape=(jax.ShapeDtypeS...  814 us

profile of v7, /device:TPU:0, one launch (start us, length us, event | category | flops | bytes accessed | tf_op | source)
XLA Modules:
  0.0 822.5 jit_solution(1840750688995534600)
XLA Ops:
  0.6 1.6 copy.8
  2.3 0.1 slice.16
  2.3 0.2 reshape.26
  2.6 0.1 reshape.24
  2.7 0.1 copy.13
  2.8 0.1 copy.10
  2.8 0.1 reduce-precision_convert_fusion.1
  3.0 0.1 fusion.1
  3.1 0.7 pad.7.wl
  3.7 814.0 %shard_map.67 = (f32[2,4,128,256]{3,2,1,0:T(8,128)}, f32[8,8,128]{2,1,0:T(8,128)}) custom-call(f32[20,512,2048]{2,1,0:T(8,128)} %bitcast.l3, f32[20,128,512]{2,1,0:T(8,128)} %bitcast.11, f32[4,512,128]{2,1,0:T(8,128)} %bitcast.15, bf16[240,256]{1,0:T(8,128)(2,1)} %pad.7.wl), custom_call_target="tpu_custom_call" | custom-call | tf_op jit(solution)/shard_map/pallas_call | solution.py:491
  817.8 1.4 slice_reduce_fusion
  819.1 1.6 copy.11
  820.7 1.8 copy.12
  (2 shorter events, 0.0 us)

commit v8 on v7

--- a/solution.py
+++ b/solution.py
@@ -61,8 +61,7 @@
         out_ref[k, 8 * i:8 * i + 8] = part
         in_ref[k, me, 8 * i:8 * i + 8] = part
 
-    @pl.loop(1, 16)
-    def _(off):
+    for off in range(1, 16):
         sum_copy(k, me, lax.rem(me + off, 16), me, *refs).start()
 
 
@@ -150,13 +149,18 @@
             vp[h, s] = vg[h, s, own, :]
         chunk = min(256, nb)
 
+        def rows_of(i):
+            return i // (nb // chunk), pl.ds(pl.multiple_of(lax.rem(i, nb // chunk) * chunk, chunk), chunk)
+
         @pl.loop(0, S * (nb // chunk))
         def _(i):
-            s = i // (nb // chunk)
-            at = pl.ds(pl.multiple_of(lax.rem(i, nb // chunk) * chunk, chunk), chunk)
-            new = (qg[h, s, at, :] - coef(0, (chunk, lt)) * vg[h, s, at, :]) * coef(1, (chunk, lt))
-            vg[h, s, at, :] = new
-            for k, v in enumerate(split3(new)):
+            s, at = rows_of(i)
+            vg[h, s, at, :] = (qg[h, s, at, :] - coef(0, (chunk, lt)) * vg[h, s, at, :]) * coef(1, (chunk, lt))
+
+        @pl.loop(0, S * (nb // chunk))
+        def _(i):
+            s, at = rows_of(i)
+            for k, v in enumerate(split3(vg[h, s, at, :])):
                 vgs[k, s, at, :] = v
 
         @pl.when(j < STEPS - 1)
@@ -346,15 +350,17 @@
         r_quarter(off, peers[off]).wait_recv()
         pass_on(off, me_l, across, rx_s, rx_r).start()
         pass_on(off, me_l, mate, rm_s, rm_r).start()
-        if off > 1:
+        if off == 2:
             for k in range(1, 4):
-                ag_copy(off - 2, k).start()
+                ag_copy(0, k).start()
     for off in range(1, 4):
         pass_on(off, across, across, rx_s, rx_r).wait_recv()
         pass_on(off, across, mate, rn_s, rn_r).start()
     for off in range(1, 4):
         pass_on(off, mate, mate, rm_s, rm_r).wait_recv()
         pass_on(off, diag, mate, rn_s, rn_r).wait_recv()
+    for k in range(1, 4):
+        ag_copy(1, k).start()
     lanes = nb // 2
     lowb = lax.broadcasted_iota(jnp.int32, (8, lanes), 0) < 4
 

time: 823 us -> 822 us (level)
  no operation moved by 1% of the time
where the time goes in v8:
time: 822 us; the launch traced here: 821 us
  Pallas kernels  813 us (99%)
    pallas_call x1, Pallas kernels, steps(): pl.pallas_call(functools.partial(kernel, cfg), out_shape=(jax.ShapeDtypeS...  813 us

profile of v8, /device:TPU:0, one launch (start us, length us, event | category | flops | bytes accessed | tf_op | source)
XLA Modules:
  0.0 821.4 jit_solution(14218916030814291066)
XLA Ops:
  0.6 1.6 copy.8
  2.3 0.1 slice.16
  2.3 0.2 reshape.26
  2.6 0.1 reshape.24
  2.7 0.1 copy.13
  2.8 0.1 copy.10
  2.8 0.1 reduce-precision_convert_fusion.1
  3.0 0.1 fusion.1
  3.1 0.7 pad.7.wl
  3.7 812.9 %shard_map.67 = (f32[2,4,128,256]{3,2,1,0:T(8,128)}, f32[8,8,128]{2,1,0:T(8,128)}) custom-call(f32[20,512,2048]{2,1,0:T(8,128)} %bitcast.l3, f32[20,128,512]{2,1,0:T(8,128)} %bitcast.11, f32[4,512,128]{2,1,0:T(8,128)} %bitcast.15, bf16[240,256]{1,0:T(8,128)(2,1)} %pad.7.wl), custom_call_target="tpu_custom_call" | custom-call | tf_op jit(solution)/shard_map/pallas_call | solution.py:497
  816.7 1.4 slice_reduce_fusion
  818.0 1.6 copy.11
  819.6 1.8 copy.12
  (2 shorter events, 0.0 us)
